TPU v7x, 32 devices: a whole 2x2x4 slice. The times are simulated.
32 devices in a mesh: band: 4 (over x, core), fft: 8 (over z, y).
Axes of the slice: x: 2, y: 2, z: 4, core: 2. Of those that a mesh axis runs over, the one named last changes fastest.
Arguments:
- orbitals: bfloat16 [16, 2, 32768], P('band', None, 'fft'), may hold values from -6 to 6
- sphere_slot: int32 [32768], P('fft'), may hold values from 0 to 24575, as said below
- stick_column: int32 [1024], P('fft'), may hold values from 0 to 36863, as said below
- potential: float32 [192, 192, 192], P('fft'), may hold values from -3 to 3
- subspace: bfloat16 [64, 2, 32768], P('band', None, 'fft'), may hold values from -0.03125 to 0.03125
- previous: bfloat16 [16, 2, 32768], P('band', None, 'fft'), may hold values from -6 to 6
Outputs:
- applied: bfloat16 [16, 2, 32768], P('band', None, 'fft')
- intersection: float32 [2, 64, 16], P(None, 'fft', 'band')
Inputs may be any that keep to these rules, and one draw needn't show every extreme that they name: `sphere_slot`: within each aligned block of 4096 entries the values are distinct. `stick_column`: aligned block d of 128 entries holds distinct columns x * 192 + y with d * 24 <= x < (d + 1) * 24.
All inputs are finite; a program needn't handle non-finite values.
Results may differ from a plain program's by a relative error of at most 0.012.
Values may be sent and summed in bfloat16 or wider, within the bound.
A program may use at most 64 MiB of HBM per device.

v0:
```python
import functools
import math

import jax
import jax.numpy as jnp
import numpy as np
from jax import lax
from jax.experimental import pallas as pl
from jax.experimental.pallas import tpu as pltpu
from jax.sharding import PartitionSpec as P


def dft_table(length, sign_value, factor):
    positions = jnp.arange(length, dtype=jnp.int32)
    phase_step = positions[:, None] * positions[None, :] % length
    angle_value = phase_step.astype(jnp.float32) * (2.0 * math.pi / length)
    cosine = (jnp.cos(angle_value) * factor).astype(jnp.bfloat16)
    sine_part = (jnp.sin(angle_value) * (sign_value * factor)).astype(jnp.bfloat16)
    return (cosine, sine_part)


def apply_dft(real_in, imag_in, table, form):
    cosine, sine_part = table

    def product(operand, table_part):
        return jnp.einsum(form, operand, table_part, preferred_element_type=jnp.float32)

    real_out = product(real_in, cosine) - product(imag_in, sine_part)
    imag_out = product(real_in, sine_part) + product(imag_in, cosine)
    return (real_out, imag_out)


def packed(pair, axis_pos):
    return jnp.stack([pair[0].astype(jnp.bfloat16), pair[1].astype(jnp.bfloat16)], axis=axis_pos)


def frequency(values, grid_size):
    return jnp.where(values >= grid_size // 2, values - grid_size, values).astype(jnp.float32)


def one_hot_rows(indices, count):
    return (indices[None, :] == jnp.arange(count, dtype=jnp.int32)[:, None]).astype(jnp.bfloat16)


def general_device(orbitals, sphere_slot, stick_column, potential, subspace, previous):
    slab_depth = potential.shape[0]
    grid_size = potential.shape[1]
    stick_count = stick_column.shape[0]
    slab_cells = slab_depth * grid_size
    forward = dft_table(grid_size, 1.0, 1.0)
    inverse = dft_table(grid_size, -1.0, 1.0 / grid_size)
    plane_index = sphere_slot // stick_count
    stick_index = sphere_slot % stick_count
    plane_hot = one_hot_rows(plane_index, grid_size)
    stick_hot = one_hot_rows(stick_index, stick_count)
    stick_coords = jnp.stack([stick_column // grid_size, stick_column % grid_size]).astype(
        jnp.bfloat16
    )
    wave_coords = jnp.dot(stick_coords, stick_hot, preferred_element_type=jnp.float32)
    freq_z = frequency(plane_index, grid_size)
    freq_x = frequency(wave_coords[0].astype(jnp.int32), grid_size)
    freq_y = frequency(wave_coords[1].astype(jnp.int32), grid_size)
    kinetic = (freq_z * freq_z + freq_x * freq_x + freq_y * freq_y) * (
        2.0 / (grid_size * grid_size)
    )
    prev_real = previous[:, 0]
    prev_imag = previous[:, 1]
    sub_piece = lax.all_gather(subspace, "band", axis=0, tiled=True)
    sub_real = sub_piece[:, 0]
    sub_imag = sub_piece[:, 1]
    over_real = jnp.einsum(
        "jg,ig->ji", sub_real, prev_real, preferred_element_type=jnp.float32
    ) + jnp.einsum("jg,ig->ji", sub_imag, prev_imag, preferred_element_type=jnp.float32)
    over_imag = jnp.einsum(
        "jg,ig->ji", sub_real, prev_imag, preferred_element_type=jnp.float32
    ) - jnp.einsum("jg,ig->ji", sub_imag, prev_real, preferred_element_type=jnp.float32)
    partial_value = jnp.stack([over_real, over_imag])
    intersection = lax.psum_scatter(partial_value, "fft", scatter_dimension=1, tiled=True)
    stick_buffer = jnp.einsum(
        "bpi,zi,si->bpzs", orbitals, plane_hot, stick_hot, preferred_element_type=jnp.float32
    ).astype(jnp.bfloat16)

    def potential_work(along_y):
        along_x = apply_dft(along_y[0], along_y[1], forward, "zxy,xk->zky")
        weighted = packed((along_x[0] * potential, along_x[1] * potential), 0)
        back_x = packed(apply_dft(weighted[0], weighted[1], inverse, "zxy,xk->zky"), 0)
        return packed(apply_dft(back_x[0], back_x[1], inverse, "zxy,yk->zxk"), 0)

    along_z = packed(apply_dft(stick_buffer[:, 0], stick_buffer[:, 1], forward, "bzs,zk->bks"), 1)
    all_columns = lax.all_gather(stick_column, "fft", axis=0, tiled=True)
    owners = all_columns.shape[0] // stick_count
    block_columns = (all_columns % slab_cells).reshape(owners, stick_count)
    block_hot = (
        block_columns[:, :, None] == jnp.arange(slab_cells, dtype=jnp.int32)[None, None, :]
    ).astype(jnp.bfloat16)

    def stick_work(one_band):
        plane_depth = one_band.shape[1]
        split_band = one_band.reshape(2, plane_depth, owners, stick_count)
        plane_grid = jnp.einsum(
            "pzds,dsc->pzdc", split_band, block_hot, preferred_element_type=jnp.float32
        ).astype(jnp.bfloat16)
        plane_grid = plane_grid.reshape(2, plane_depth, grid_size, grid_size)
        along_y = packed(apply_dft(plane_grid[0], plane_grid[1], forward, "zxy,yk->zxk"), 0)
        back_y = potential_work(along_y)
        back_split = back_y.reshape(2, plane_depth, owners, slab_cells)
        picked = jnp.einsum(
            "pzdc,dsc->pzds", back_split, block_hot, preferred_element_type=jnp.float32
        ).astype(jnp.bfloat16)
        return picked.reshape(2, plane_depth, owners * stick_count)

    finished = lax.map(
        stick_work, lax.all_to_all(along_z, "fft", split_axis=2, concat_axis=3, tiled=True)
    )
    stick_values = lax.all_to_all(finished, "fft", split_axis=3, concat_axis=2, tiled=True)
    picked_sticks = jnp.einsum(
        "bpzs,si->bpzi", stick_values, stick_hot, preferred_element_type=jnp.float32
    ).astype(jnp.bfloat16)
    cosine_cols = jnp.einsum("zk,ki->zi", inverse[0], plane_hot, preferred_element_type=jnp.float32)
    sine_cols = jnp.einsum("zk,ki->zi", inverse[1], plane_hot, preferred_element_type=jnp.float32)
    pick_real = picked_sticks[:, 0].astype(jnp.float32)
    pick_imag = picked_sticks[:, 1].astype(jnp.float32)
    wave_real = jnp.sum(pick_real * cosine_cols[None] - pick_imag * sine_cols[None], axis=1)
    wave_imag = jnp.sum(pick_real * sine_cols[None] + pick_imag * cosine_cols[None], axis=1)
    real_out = wave_real + kinetic * orbitals[:, 0].astype(jnp.float32)
    imag_out = wave_imag + kinetic * orbitals[:, 1].astype(jnp.float32)
    applied = jnp.stack([real_out, imag_out], axis=1).astype(jnp.bfloat16)
    return (applied, intersection)


PLANES = 4
EXTRA = 16
LANES = 128


def phases(products, length):
    angle = (products % length).astype(np.float64) * (2.0 * np.pi / length)
    return np.cos(angle), np.sin(angle)


def line_tables(length):
    cosine, sine = phases(np.outer(np.arange(length), np.arange(length)), length)
    wide = -(-length // 128) * 128
    empty = np.zeros((length, wide - length))
    from_real = np.concatenate([cosine, empty, sine, empty], axis=1)
    from_imag = np.concatenate([-sine, empty, cosine, empty], axis=1)
    return jnp.asarray(np.stack([from_real, from_imag]), jnp.bfloat16)


def half_tables(length):
    half = np.arange(length // 2)
    tables = []
    for parity in (0, 1):
        cosine, sine = phases(np.outer(2 * half + parity, half), length)
        tables.append(np.block([[cosine, -sine], [sine, cosine]]))
    tables.extend([tables[0].T, tables[1].T])
    return jnp.asarray(np.stack(tables), jnp.bfloat16)


def column_tables(length):
    cosine, sine = phases(np.outer(np.arange(length), np.arange(length)), length)
    there = np.block([[cosine, -sine], [sine, cosine]])
    return jnp.asarray(there, jnp.bfloat16), jnp.asarray(there.T, jnp.bfloat16)


def plane_kernel(
    slab,
    sent_ref,
    pot_ref,
    line_ref,
    half_ref,
    extra_ref,
    back_ref,
    stick_ref,
    rows_ref,
    real_ref,
    imag_ref,
    after_real_ref,
    after_imag_ref,
    left_ref,
    right_ref,
    stage_ref,
    send_sem,
    recv_sem,
):
    owners, _, sticks = sent_ref.shape
    lines, size, _ = real_ref.shape
    half = size // 2
    wide = line_ref.shape[2] // 2
    groups = slab // PLANES
    part_rows = groups * lines
    me = lax.axis_index("fft")
    others = [lax.rem(me + shift, owners) for shift in range(1, owners)]
    scale = 1.0 / (size * size)

    def stick_mask(owner):
        coords = stick_ref[owner, 2 * part_rows : 2 * part_rows + EXTRA, :].astype(jnp.float32)
        local = lax.broadcasted_iota(jnp.int32, (slab, sticks), 0).astype(jnp.float32)
        return coords[0:1, :] == local

    def plane_group(group):
        first = pl.multiple_of(group * lines, lines)
        second = pl.multiple_of(part_rows + group * lines, lines)

        @pl.loop(0, owners, unroll=2)
        def _(owner):
            mask = stick_mask(owner)[None]
            spread = []
            for start in (first, second):
                values = stick_ref[owner, pl.ds(start, lines), :].astype(jnp.float32)
                spread.append(
                    jnp.where(mask, values[:, None, :], 0.0).reshape(lines * slab, sticks)
                )
            left = jnp.concatenate(spread, axis=1).astype(jnp.bfloat16)
            result = jnp.dot(left, rows_ref[owner], preferred_element_type=jnp.float32)
            place = pl.ds(pl.multiple_of(owner * slab, 8), slab)
            real_ref[:, place, :] = result[:, :size].reshape(lines, slab, size)
            imag_ref[:, place, :] = result[:, wide : wide + size].reshape(lines, slab, size)

        def one_plane(line, plane):
            real_low, real_high = real_ref[line, :half, :], real_ref[line, half:, :]
            imag_low, imag_high = imag_ref[line, :half, :], imag_ref[line, half:, :]
            total = jnp.concatenate([real_low + real_high, imag_low + imag_high], axis=0)
            differ = jnp.concatenate([real_low - real_high, imag_low - imag_high], axis=0)

            def there_and_back(values, parity):
                forward = jnp.dot(
                    half_ref[parity],
                    values.astype(jnp.bfloat16),
                    preferred_element_type=jnp.float32,
                )
                picks = pl.ds(parity, half, 2)
                local = jnp.concatenate(
                    [left_ref[plane, picks, :], right_ref[plane, picks, :][:, : size - LANES]], axis=1
                )
                weighted = jnp.concatenate([forward[:half] * local, forward[half:] * local], axis=0)
                return jnp.dot(
                    half_ref[2 + parity],
                    weighted.astype(jnp.bfloat16),
                    preferred_element_type=jnp.float32,
                )

            even = there_and_back(total, 0)
            odd = there_and_back(differ, 1)
            low, high = even + odd, even - odd
            after_real_ref[line, :half, :] = low[:half]
            after_imag_ref[line, :half, :] = low[half:]
            after_real_ref[line, half:, :] = high[:half]
            after_imag_ref[line, half:, :] = high[half:]

        bands = lines // PLANES

        @pl.loop(0, PLANES)
        def _(plane):
            whole_plane = group * PLANES + plane
            left_ref[plane] = pot_ref[whole_plane, :, :LANES]
            right_ref[plane, :, : size - LANES] = pot_ref[whole_plane, :, LANES:]
            for band in range(bands):
                one_plane(plane * bands + band, plane)

        @pl.loop(0, owners, unroll=2)
        def _(owner):
            mask = stick_mask(owner)[None]
            place = pl.ds(pl.multiple_of(owner * slab, 8), slab)
            real = after_real_ref[:, place, :].reshape(lines * slab, size).astype(jnp.bfloat16)
            imag = after_imag_ref[:, place, :].reshape(lines * slab, size).astype(jnp.bfloat16)
            across = (((1,), (1,)), ((), ()))
            result = lax.dot_general(
                real, rows_ref[owner, :, :size], across, preferred_element_type=jnp.float32
            ) + lax.dot_general(
                imag,
                rows_ref[owner, :, wide : wide + size],
                across,
                preferred_element_type=jnp.float32,
            )
            result = result.reshape(lines, slab, 2 * sticks)
            for part in range(2):
                chosen = result[:, :, part * sticks : (part + 1) * sticks]
                picked = jnp.sum(jnp.where(mask, chosen, 0.0), axis=1) * scale
                start = pl.multiple_of((2 * group + part) * lines, lines)
                stage_ref[owner, pl.ds(start, lines), :] = picked.astype(jnp.bfloat16)

    def rows_of(group):
        return pl.ds(pl.multiple_of(group * 2 * lines, 2 * lines), 2 * lines)

    def group_copy(group, place):
        return pltpu.make_async_remote_copy(
            src_ref=stage_ref.at[others[place], rows_of(group)],
            dst_ref=back_ref.at[me, rows_of(group)],
            send_sem=send_sem.at[group, place],
            recv_sem=recv_sem.at[group, place],
            device_id={"fft": others[place]},
            device_id_type=pl.DeviceIdType.MESH,
        )

    def extra_copy(place):
        return pltpu.make_async_remote_copy(
            src_ref=extra_ref.at[others[place]],
            dst_ref=back_ref.at[me, pl.ds(2 * part_rows, EXTRA)],
            send_sem=send_sem.at[groups, place],
            recv_sem=recv_sem.at[groups, place],
            device_id={"fft": others[place]},
            device_id_type=pl.DeviceIdType.MESH,
        )

    def stick_copy(place):
        return pltpu.make_async_remote_copy(
            src_ref=sent_ref.at[others[place]],
            dst_ref=stick_ref.at[me],
            send_sem=send_sem.at[groups + 1, place],
            recv_sem=recv_sem.at[groups + 1, place],
            device_id={"fft": others[place]},
            device_id_type=pl.DeviceIdType.MESH,
        )

    barrier = pltpu.get_barrier_semaphore()
    for other in others:
        pl.semaphore_signal(
            barrier, inc=1, device_id={"fft": other}, device_id_type=pl.DeviceIdType.MESH
        )

    pl.semaphore_wait(barrier, owners - 1)
    for place in range(owners - 1):
        stick_copy(place).start()
    for place in range(owners - 1):
        extra_copy(place).start()
    stick_ref[me] = sent_ref[me]
    for place in range(owners - 1):
        stick_copy(place).wait()

    @pl.loop(0, owners)
    def _(owner):
        coords = stick_ref[owner, 2 * part_rows : 2 * part_rows + EXTRA, :].astype(jnp.float32)
        cells = lax.broadcasted_iota(jnp.int32, (size, sticks), 0).astype(jnp.float32)
        hot = jnp.where(coords[1:2, :] == cells, 1.0, 0.0).astype(jnp.bfloat16)
        for part in range(2):
            rows = lax.dot_general(
                hot,
                line_ref[part],
                (((0,), (0,)), ((), ())),
                preferred_element_type=jnp.float32,
            )
            rows_ref[owner, part * sticks : (part + 1) * sticks, :] = rows.astype(jnp.bfloat16)

    @pl.loop(0, groups)
    def _(group):
        plane_group(group)
        for place in range(owners - 1):
            group_copy(group, place).start()

    back_ref[me, : 2 * part_rows, :] = stage_ref[me]
    back_ref[me, 2 * part_rows :, :] = extra_ref[me]
    for place in range(owners - 1):
        extra_copy(place).wait()

    @pl.loop(0, groups)
    def _(group):
        for place in range(owners - 1):
            group_copy(group, place).wait()


def plane_work(sent, potential, extra, bands):
    owners, _, sticks = sent.shape
    slab, size, _ = potential.shape
    lines = PLANES * bands
    groups = slab // PLANES
    lines_table = line_tables(size)
    halves = half_tables(size)
    wide = lines_table.shape[2]
    rows = 2 * slab * bands
    in_vmem = pl.BlockSpec(memory_space=pltpu.VMEM)
    grid_part = pltpu.VMEM((lines, size, size), jnp.float32)
    return pl.pallas_call(
        functools.partial(plane_kernel, slab),
        out_shape=jax.ShapeDtypeStruct((owners, rows + EXTRA, sticks), jnp.bfloat16),
        in_specs=[in_vmem] * 5,
        out_specs=in_vmem,
        scratch_shapes=[
            pltpu.VMEM((owners, rows + EXTRA, sticks), jnp.bfloat16),
            pltpu.VMEM((owners, 2 * sticks, wide), jnp.bfloat16),
            grid_part,
            grid_part,
            grid_part,
            grid_part,
            pltpu.VMEM((PLANES, size, LANES), jnp.float32),
            pltpu.VMEM((PLANES, size, LANES), jnp.float32),
            pltpu.VMEM((owners, rows, sticks), jnp.bfloat16),
            pltpu.SemaphoreType.DMA((groups + 2, owners - 1)),
            pltpu.SemaphoreType.DMA((groups + 2, owners - 1)),
        ],
        compiler_params=pltpu.CompilerParams(
            collective_id=0, has_side_effects=True, vmem_limit_bytes=48 * 1024 * 1024
        ),
        cost_estimate=pl.CostEstimate(
            flops=40 * 10**9, bytes_accessed=8 * 10**6, transcendentals=0
        ),
    )(sent, potential, lines_table, halves, extra)


def gathered_bands(array, mesh_bands):
    here = lax.axis_index("band")
    blocks = [array]
    for shift in range(1, mesh_bands):
        pairs = [((src + shift) % mesh_bands, src) for src in range(mesh_bands)]
        blocks.append(lax.ppermute(array, "band", pairs))
    return blocks, here


def overlaps(subspace, previous, mesh_bands, owners):
    blocks, here = gathered_bands(subspace, mesh_bands)
    prev_real, prev_imag = previous[:, 0], previous[:, 1]
    right = jnp.concatenate(
        [
            jnp.concatenate([prev_real, prev_imag], axis=1),
            jnp.concatenate([prev_imag, -prev_real], axis=1),
        ],
        axis=0,
    )
    partials = []
    for block in blocks:
        partials.append(
            jnp.einsum(
                "jg,ig->ji",
                block.reshape(block.shape[0], -1),
                right,
                preferred_element_type=jnp.float32,
            )
        )
    twice = jnp.concatenate(partials + partials, axis=0)
    count = twice.shape[0] // 2
    start = (count - here * subspace.shape[0]) % count
    ordered = lax.dynamic_slice_in_dim(twice, start, count, axis=0)
    split = ordered.reshape(owners, count // owners, 2, previous.shape[0])
    return split.transpose(0, 2, 1, 3)


def fast_device(mesh_bands, orbitals, sphere_slot, stick_column, potential, subspace, previous):
    slab_depth, grid_size, _ = potential.shape
    stick_count = stick_column.shape[0]
    owners = grid_size // slab_depth
    bands = orbitals.shape[0]
    plane_index = sphere_slot // stick_count
    stick_index = sphere_slot % stick_count
    plane_hot = one_hot_rows(plane_index, grid_size)
    stick_hot = one_hot_rows(stick_index, stick_count)
    stick_x = stick_column // grid_size
    stick_y = stick_column % grid_size
    stick_coords = jnp.stack([stick_x, stick_y]).astype(jnp.bfloat16)
    wave_coords = jnp.dot(stick_coords, stick_hot, preferred_element_type=jnp.float32)
    freq_z = frequency(plane_index, grid_size)
    freq_x = frequency(wave_coords[0].astype(jnp.int32), grid_size)
    freq_y = frequency(wave_coords[1].astype(jnp.int32), grid_size)
    kinetic = (freq_z * freq_z + freq_x * freq_x + freq_y * freq_y) * (
        2.0 / (grid_size * grid_size)
    )
    local_x = stick_x - lax.axis_index("fft") * slab_depth
    coords = jnp.stack([local_x, stick_y]).astype(jnp.bfloat16)
    coords = jnp.pad(coords, ((0, EXTRA - 2), (0, 0)))
    coords = jnp.broadcast_to(coords[None], (owners, EXTRA, stick_count))
    stick_buffer = jnp.einsum(
        "bpi,zi,si->pzbs", orbitals, plane_hot, stick_hot, preferred_element_type=jnp.float32
    ).astype(jnp.bfloat16)
    forward, backward = column_tables(grid_size)
    along_z = jnp.dot(
        forward,
        stick_buffer.reshape(2 * grid_size, bands * stick_count),
        preferred_element_type=jnp.float32,
    ).astype(jnp.bfloat16)
    along_z = along_z.reshape(2, owners, slab_depth * bands, stick_count)
    pieces = [along_z[0], along_z[1]]
    sent = jnp.concatenate(pieces + [coords], axis=1)
    split = overlaps(subspace, previous, mesh_bands, owners)
    flat = split.reshape(owners, 1, -1)
    high = lax.reduce_precision(flat, 8, 7)
    low = lax.reduce_precision(flat - high, 8, 7)
    both = jnp.concatenate([high, low], axis=2).astype(jnp.bfloat16)
    width = both.shape[2]
    lanes = -(-width // stick_count) * stick_count
    both = jnp.pad(both, ((0, 0), (0, 0), (0, lanes - width)))
    both = both.reshape(owners, -1, stick_count)
    both = jnp.pad(both, ((0, 0), (0, EXTRA - both.shape[1]), (0, 0)))
    returned = plane_work(sent, potential, both, bands)
    rows = 2 * slab_depth * bands
    sums = returned[:, rows:].reshape(owners, -1)[:, :width].astype(jnp.float32)
    sums = jnp.sum(sums, axis=0)
    intersection = (sums[: width // 2] + sums[width // 2 :]).reshape(split.shape[1:])
    stick_values = returned[:, :rows].reshape(owners, -1, 2, PLANES, bands * stick_count)
    stick_values = stick_values.transpose(2, 0, 1, 3, 4).reshape(2 * grid_size, -1)
    columns = jnp.dot(backward, stick_values, preferred_element_type=jnp.float32)
    columns = (columns * (1.0 / grid_size)).astype(jnp.bfloat16)
    columns = columns.reshape(2, grid_size, bands, stick_count)
    picked = jnp.einsum(
        "pzbs,si->pzbi", columns, stick_hot, preferred_element_type=jnp.float32
    ).astype(jnp.bfloat16)
    levels = jnp.arange(grid_size, dtype=jnp.int32)[:, None]
    here = (plane_index[None, :] == levels)[None, :, None, :]
    waves = jnp.sum(jnp.where(here, picked.astype(jnp.float32), 0.0), axis=1)
    wave_real, wave_imag = waves[0], waves[1]
    real_out = wave_real + kinetic * orbitals[:, 0].astype(jnp.float32)
    imag_out = wave_imag + kinetic * orbitals[:, 1].astype(jnp.float32)
    applied = jnp.stack([real_out, imag_out], axis=1).astype(jnp.bfloat16)
    return (applied, intersection)


def per_device(mesh_bands, *arrays):
    orbitals, _, _, potential, _, previous = arrays
    slab_depth = potential.shape[0]
    bands = orbitals.shape[0]
    aligned = slab_depth % 8 == 0 and slab_depth % PLANES == 0
    aligned = aligned and LANES < potential.shape[1] <= 2 * LANES
    if aligned and PLANES * bands % 16 == 0 and arrays[2].shape[0] % 128 == 0:
        return fast_device(mesh_bands, *arrays)
    return general_device(*arrays)


def solution(mesh):
    return jax.shard_map(
        functools.partial(per_device, mesh.shape["band"]),
        mesh=mesh,
        in_specs=(
            P("band", None, "fft"),
            P("fft"),
            P("fft"),
            P("fft", None, None),
            P("band", None, "fft"),
            P("band", None, "fft"),
        ),
        out_specs=(P("band", None, "fft"), P(None, "fft", "band")),
        check_vma=False,
    )
```

profile of v0, /device:TPU:0, one launch (start us, length us, event | category | flops | bytes accessed | tf_op | source)
XLA Modules:
  0.0 88.4 jit_solution(2847232542889917228)
XLA Ops:
  0.6 0.5 collective-permute-start.2
  1.2 2.6 %collective-permute-start.1 = (bf16[16,2,4096]{2,1,0:T(2,128)(2,1)}, bf16[16,2,4096]{2,1,0:T(2,128)(2,1)S(1)}, u32[]{:S(2)}, u32[]{:S(2)}) collective-permute-start(bf16[16,2,4096]{2,1,0:T(2,128)(2,1)} %param.14), channel_id=1, source_target_pairs={{16,0},{24,8},{0,16},{8,24},{17,1},{25,9},{1,17},{9,25},{18,2},{26... | collective-permute-start | bytes 786440 | tf_op jit(solution)/shard_map/ppermute | solution.py:405
  3.7 1.4 %collective-permute-start = (bf16[16,2,4096]{2,1,0:T(2,128)(2,1)}, bf16[16,2,4096]{2,1,0:T(2,128)(2,1)S(1)}, u32[]{:S(2)}, u32[]{:S(2)}) collective-permute-start(bf16[16,2,4096]{2,1,0:T(2,128)(2,1)} %param.14), channel_id=1, source_target_pairs={{8,0},{16,8},{24,16},{0,24},{9,1},{17,9},{25,17},{1,25},{10,2},{18... | collective-permute-start | bytes 786440 | tf_op jit(solution)/shard_map/ppermute | solution.py:405
  5.1 0.9 %convert_bitcast_fusion.1 = f32[4096,4,2]{0,2,1:T(2,128)S(1)} fusion(bf16[4,2,4096]{2,1,0:T(2,128)(2,1)} %param.10), kind=kLoop, calls=%fused_computation.30 | loop fusion | flops 32768 | bytes 196608 | tf_op jit(solution)/shard_map/convert.5
  6.0 1.7 %fusion.57 = (bf16[4,1,4096]{2,1,0:T(2,128)(2,1)S(1)}, bf16[4,1,4096]{2,1,0:T(2,128)(2,1)}) fusion(bf16[4,2,4096]{2,1,0:T(2,128)(2,1)} %param.10), kind=kLoop, calls=%fused_computation.90 | loop fusion | bytes 131072 | tf_op jit(solution)/shard_map/slice | solution.py:499
  7.7 1.0 %fusion.58 = (bf16[4,1,4096]{2,1,0:T(2,128)(2,1)S(1)}, bf16[4,1,4096]{2,1,0:T(2,128)(2,1)S(1)}) fusion(bf16[4,2,4096]{2,1,0:T(2,128)(2,1)} %param.15), kind=kLoop, calls=%fused_computation.91 | loop fusion | bytes 131072 | tf_op jit(solution)/shard_map/slice | solution.py:411
  8.7 0.1 fusion.55
  8.8 0.0 copy-start.6
  8.8 1.1 %copy.70 = bf16[2,8,2,4096]{3,1,2,0:T(8,128)(2,1)S(1)} copy(bf16[2,8,2,4096]{3,2,1,0:T(2,128)(2,1)} %bitcast.101) | data formatting | bytes 524288
  9.9 0.7 add_select_fusion
  10.7 0.2 convert_bitcast_fusion
  10.9 0.4 iota_compare_fusion
  11.3 0.0 copy-start.3
  11.3 2.9 %fusion.16 = bf16[2,192,4,128]{3,1,0,2:T(8,128)(2,1)S(1)} fusion(f32[4096,4,2]{0,2,1:T(2,128)S(1)} %convert_bitcast_fusion.1, f32[4096,128]{0,1:T(8,128)S(1)} %convert_bitcast_fusion, s32[4096]{0:T(1024)S(1)} %get-tuple-element.27), kind=kOutput, calls=%fused_computation.17 | convolution fusion | flops 1615790080 | bytes 2637824 | tf_op jit(solution)/shard_map/bpi,zi,si->pzbs/dot_general | solution.py:460
  14.2 0.0 copy-start.8
  14.2 0.0 copy-start.5
  14.2 0.3 copy.48
  14.5 0.0 copy-done.3
  14.6 0.4 fusion.15
  15.0 0.1 squeeze.22
  15.1 0.0 copy-start
  15.1 0.0 copy-start.1
  15.1 0.1 squeeze.23
  15.3 0.0 copy-done.8
  15.3 0.4 fusion.6
  15.8 0.0 copy-done.6
  15.8 0.2 convolution_bitcast_fusion.3
  16.0 0.0 copy-start.7
  16.0 0.0 copy-done.5
  16.1 0.0 collective-permute-done.2
  16.1 0.2 copy.73
  16.3 1.0 %convolution_bitcast_fusion = f32[16,8]{0,1:T(8,128)S(1)} fusion(bf16[16,8192]{1,0:T(8,128)(2,1)S(1)} %bitcast.107, bf16[4,4096]{1,0:T(4,128)(2,1)S(1)} %get-tuple-element.14, bf16[4,4096]{1,0:T(4,128)(2,1)S(1)} %bitcast.115, bf16[4,4096]{1,0:T(4,128)(2,1)} %copy-done.6), kind=kOutput, calls=%fused_computation.19 | convolution fusion | flops 2621440 | bytes 360960 | tf_op jit(solution)/shard_map/jg,ig->ji/dot_general | solution.py:422
  17.3 0.0 collective-permute-done.1
  17.3 0.2 copy.72
  17.4 1.0 %convolution_bitcast_fusion.1 = f32[16,8]{0,1:T(8,128)S(1)} fusion(bf16[16,8192]{1,0:T(8,128)(2,1)S(1)} %bitcast.108, bf16[4,4096]{1,0:T(4,128)(2,1)S(1)} %get-tuple-element.14, bf16[4,4096]{1,0:T(4,128)(2,1)S(1)} %bitcast.116, bf16[4,4096]{1,0:T(4,128)(2,1)} %copy-done.6), kind=kOutput, calls=%fused_computation.20 | convolution fusion | flops 2621440 | bytes 360960 | tf_op jit(solution)/shard_map/jg,ig->ji/dot_general | solution.py:422
  18.4 0.0 collective-permute-done
  18.4 0.2 copy.71
  18.5 0.0 copy-done.7
  18.6 0.2 convolution_bitcast_fusion.2
  18.8 0.1 concatenate.35
  18.8 0.1 constant_dynamic-slice_fusion
  18.9 0.1 reshape.146
  19.0 0.1 copy.50
  19.1 0.1 copy.51
  19.2 0.1 fusion.33.extra_ref
  19.3 0.0 copy-done
  19.3 0.0 copy-done.1
  19.3 0.0 copy-start.2
  19.3 62.2 %shard_map.113 = bf16[8,208,128]{2,1,0:T(8,128)(2,1)S(1)} custom-call(bf16[8,208,128]{2,1,0:T(8,128)(2,1)S(1)} %pad_maximum_fusion.sent_ref, f32[24,192,192]{2,1,0:T(8,128)} %pot_ref.1, bf16[2,192,512]{2,1,0:T(8,128)(2,1)S(1)} %copy-done, bf16[4,192,192]{2,1,0:T(8,128)(2,1)S(1)} %copy-done.1, bf16[8,16,128]{2,1,0:T(8,128)(2,1)S(1)} %fusion.33.extra_ref), custom_call_target="tpu_custom_call" | custom-call | flops 40000000000 | bytes 8000000 | tf_op jit(solution)/shard_map/pallas_call | solution.py:373
  81.5 0.2 reshape.152
  81.8 0.0 copy-done.2
  81.8 0.5 fusion.21
  82.2 0.3 reshape.159
  82.5 0.0 copy-start.4
  82.5 4.1 %select_reduce_fusion = f32[2,4,4096]{2,1,0:T(4,128)S(1)} fusion(pred[192,4096]{1,0:T(8,128)(4,1)S(1)} %iota_compare_fusion, s32[4096]{0:T(1024)S(1)} %get-tuple-element.26, bf16[2,192,4,128]{1,0,3,2:T(2,128)(2,1)S(1)} %reshape.159), kind=kOutput, calls=%fused_computation | convolution fusion | flops 1636270080 | bytes 1327104 | tf_op jit(solution)/shard_map/pzbs,si->pzbi/dot_general | solution.py:492
  86.6 0.0 copy-done.4
  86.6 0.1 fusion.30
  86.8 0.7 copy.59
  87.6 0.1 slice_add_fusion
  87.6 0.1 add.58
  87.7 0.7 copy.60
  (18 shorter events, 0.4 us)
Async XLA Ops:
  0.6 15.5 %collective-permute-start.2 = (bf16[16,2,4096]{2,1,0:T(2,128)(2,1)}, bf16[16,2,4096]{2,1,0:T(2,128)(2,1)S(1)}, u32[]{:S(2)}, u32[]{:S(2)}) collective-permute-start(bf16[16,2,4096]{2,1,0:T(2,128)(2,1)} %param.14), channel_id=1, source_target_pairs={{24,0},{0,8},{8,16},{16,24},{25,1},{1,9},{9,17},{17,25},{26,2},{2,... | collective-permute-start | bytes 786440 | tf_op jit(solution)/shard_map/ppermute | solution.py:405
  1.2 16.1 %collective-permute-start.1 = (bf16[16,2,4096]{2,1,0:T(2,128)(2,1)}, bf16[16,2,4096]{2,1,0:T(2,128)(2,1)S(1)}, u32[]{:S(2)}, u32[]{:S(2)}) collective-permute-start(bf16[16,2,4096]{2,1,0:T(2,128)(2,1)} %param.14), channel_id=1, source_target_pairs={{16,0},{24,8},{0,16},{8,24},{17,1},{25,9},{1,17},{9,25},{18,2},{26... | collective-permute-start | bytes 786440 | tf_op jit(solution)/shard_map/ppermute | solution.py:405
  3.7 14.7 %collective-permute-start = (bf16[16,2,4096]{2,1,0:T(2,128)(2,1)}, bf16[16,2,4096]{2,1,0:T(2,128)(2,1)S(1)}, u32[]{:S(2)}, u32[]{:S(2)}) collective-permute-start(bf16[16,2,4096]{2,1,0:T(2,128)(2,1)} %param.14), channel_id=1, source_target_pairs={{8,0},{16,8},{24,16},{0,24},{9,1},{17,9},{25,17},{1,25},{10,2},{18... | collective-permute-start | bytes 786440 | tf_op jit(solution)/shard_map/ppermute | solution.py:405
  8.8 7.0 %copy-start.6 = (bf16[4,4096]{1,0:T(4,128)(2,1)}, bf16[4,4096]{1,0:T(4,128)(2,1)S(1)}, u32[]{:S(2)}) copy-start(bf16[4,4096]{1,0:T(4,128)(2,1)S(1)} %get-tuple-element.15) | copy-start | bytes 98308
  11.3 3.2 %copy-start.3 = (bf16[384,384]{1,0:T(8,128)(2,1)S(1)}, bf16[384,384]{1,0:T(8,128)(2,1)}, u32[]{:S(2)}) copy-start(bf16[384,384]{1,0:T(8,128)(2,1)} %constant.93.clone) | copy-start | bytes 884740
  14.2 1.1 %copy-start.8 = (s32[128]{0:T(128)S(1)}, s32[128]{0:T(128)}, u32[]{:S(2)}) copy-start(s32[128]{0:T(128)} %param.12) | copy-start | bytes 1540
  14.2 1.8 %copy-start.5 = (s32[4096]{0:T(1024)S(1)}, s32[4096]{0:T(1024)}, u32[]{:S(2)}) copy-start(s32[4096]{0:T(1024)} %param.11) | copy-start | bytes 49156
  15.1 4.2 %copy-start = (bf16[2,192,512]{2,1,0:T(8,128)(2,1)S(1)}, bf16[2,192,512]{2,1,0:T(8,128)(2,1)}, u32[]{:S(2)}) copy-start(bf16[2,192,512]{2,1,0:T(8,128)(2,1)} %constant.95.clone.line_ref) | copy-start | bytes 1179652
  15.1 4.2 %copy-start.1 = (bf16[4,192,192]{2,1,0:T(8,128)(2,1)S(1)}, bf16[4,192,192]{2,1,0:T(8,128)(2,1)}, u32[]{:S(2)}) copy-start(bf16[4,192,192]{2,1,0:T(8,128)(2,1)} %constant.96.clone.half_ref) | copy-start | bytes 884740
  16.0 2.5 %copy-start.7 = (bf16[4,4096]{1,0:T(4,128)(2,1)S(1)}, bf16[4,4096]{1,0:T(4,128)(2,1)}, u32[]{:S(2)}) copy-start(bf16[4,4096]{1,0:T(4,128)(2,1)} %copy-done.6) | copy-start | bytes 98308
  19.3 62.5 %copy-start.2 = (bf16[384,384]{1,0:T(8,128)(2,1)S(1)}, bf16[384,384]{1,0:T(8,128)(2,1)}, u32[]{:S(2)}) copy-start(bf16[384,384]{1,0:T(8,128)(2,1)} %constant.103) | copy-start | bytes 884740
  82.5 4.1 %copy-start.4 = (bf16[4,1,4096]{2,1,0:T(2,128)(2,1)S(1)}, bf16[4,1,4096]{2,1,0:T(2,128)(2,1)}, u32[]{:S(2)}) copy-start(bf16[4,1,4096]{2,1,0:T(2,128)(2,1)} %get-tuple-element.21) | copy-start | bytes 98308
where the time goes:
time: 88.9 us; the launch traced here: 88.4 us
  Pallas kernels  62.2 us (70%)
  matrix products  10.5 us (12%)
  local copies, waits for them, and re-layouts  7.41 us (8%)
  starting transfers between devices  4.48 us (5%)
  other arithmetic  2.78 us (3%)
  between operations  1.01 us (1%)
    pallas_call x1, Pallas kernels, plane_work(): pl.pallas_call(functools.partial(plane_kernel, slab), out_shape=jax.Shape...  62.2 us
    ppermute x3, starting transfers between devices, gathered_bands(): blocks.append(lax.ppermute(array, 'band', pairs))  4.48 us
    dot_general x1, matrix products, fast_device(): jnp.einsum('pzbs,si->pzbi', columns, stick_hot, preferred_element_type=jn...  4.08 us
    unnamed x27, local copies, waits for them, and re-layouts  3.07 us
    dot_general x1, matrix products, fast_device(): jnp.einsum('bpi,zi,si->pzbs', orbitals, plane_hot, stick_hot, preferred_e...  2.87 us
    dot_general x4, matrix products, overlaps(): jnp.einsum('jg,ig->ji', block.reshape(block.shape[0], -1), right, preferr...  2.33 us
  transfers between devices with their start and end apart: 3, of which 0 were waited for; matrix products, arithmetic and copies ran while one was open for 15% of the time, Pallas kernels for 0%

commit v1 on v0

v1 whole, which is shorter than its diff:
```python
import functools
import math

import jax
import jax.numpy as jnp
import numpy as np
from jax import lax
from jax.experimental import pallas as pl
from jax.experimental.pallas import tpu as pltpu
from jax.sharding import PartitionSpec as P


def dft_table(length, sign_value, factor):
    positions = jnp.arange(length, dtype=jnp.int32)
    phase_step = positions[:, None] * positions[None, :] % length
    angle_value = phase_step.astype(jnp.float32) * (2.0 * math.pi / length)
    cosine = (jnp.cos(angle_value) * factor).astype(jnp.bfloat16)
    sine_part = (jnp.sin(angle_value) * (sign_value * factor)).astype(jnp.bfloat16)
    return (cosine, sine_part)


def apply_dft(real_in, imag_in, table, form):
    cosine, sine_part = table

    def product(operand, table_part):
        return jnp.einsum(form, operand, table_part, preferred_element_type=jnp.float32)

    real_out = product(real_in, cosine) - product(imag_in, sine_part)
    imag_out = product(real_in, sine_part) + product(imag_in, cosine)
    return (real_out, imag_out)


def packed(pair, axis_pos):
    return jnp.stack([pair[0].astype(jnp.bfloat16), pair[1].astype(jnp.bfloat16)], axis=axis_pos)


def frequency(values, grid_size):
    return jnp.where(values >= grid_size // 2, values - grid_size, values).astype(jnp.float32)


def one_hot_rows(indices, count):
    return (indices[None, :] == jnp.arange(count, dtype=jnp.int32)[:, None]).astype(jnp.bfloat16)


def general_device(orbitals, sphere_slot, stick_column, potential, subspace, previous):
    slab_depth = potential.shape[0]
    grid_size = potential.shape[1]
    stick_count = stick_column.shape[0]
    slab_cells = slab_depth * grid_size
    forward = dft_table(grid_size, 1.0, 1.0)
    inverse = dft_table(grid_size, -1.0, 1.0 / grid_size)
    plane_index = sphere_slot // stick_count
    stick_index = sphere_slot % stick_count
    plane_hot = one_hot_rows(plane_index, grid_size)
    stick_hot = one_hot_rows(stick_index, stick_count)
    stick_coords = jnp.stack([stick_column // grid_size, stick_column % grid_size]).astype(
        jnp.bfloat16
    )
    wave_coords = jnp.dot(stick_coords, stick_hot, preferred_element_type=jnp.float32)
    freq_z = frequency(plane_index, grid_size)
    freq_x = frequency(wave_coords[0].astype(jnp.int32), grid_size)
    freq_y = frequency(wave_coords[1].astype(jnp.int32), grid_size)
    kinetic = (freq_z * freq_z + freq_x * freq_x + freq_y * freq_y) * (
        2.0 / (grid_size * grid_size)
    )
    prev_real = previous[:, 0]
    prev_imag = previous[:, 1]
    sub_piece = lax.all_gather(subspace, "band", axis=0, tiled=True)
    sub_real = sub_piece[:, 0]
    sub_imag = sub_piece[:, 1]
    over_real = jnp.einsum(
        "jg,ig->ji", sub_real, prev_real, preferred_element_type=jnp.float32
    ) + jnp.einsum("jg,ig->ji", sub_imag, prev_imag, preferred_element_type=jnp.float32)
    over_imag = jnp.einsum(
        "jg,ig->ji", sub_real, prev_imag, preferred_element_type=jnp.float32
    ) - jnp.einsum("jg,ig->ji", sub_imag, prev_real, preferred_element_type=jnp.float32)
    partial_value = jnp.stack([over_real, over_imag])
    intersection = lax.psum_scatter(partial_value, "fft", scatter_dimension=1, tiled=True)
    stick_buffer = jnp.einsum(
        "bpi,zi,si->bpzs", orbitals, plane_hot, stick_hot, preferred_element_type=jnp.float32
    ).astype(jnp.bfloat16)

    def potential_work(along_y):
        along_x = apply_dft(along_y[0], along_y[1], forward, "zxy,xk->zky")
        weighted = packed((along_x[0] * potential, along_x[1] * potential), 0)
        back_x = packed(apply_dft(weighted[0], weighted[1], inverse, "zxy,xk->zky"), 0)
        return packed(apply_dft(back_x[0], back_x[1], inverse, "zxy,yk->zxk"), 0)

    along_z = packed(apply_dft(stick_buffer[:, 0], stick_buffer[:, 1], forward, "bzs,zk->bks"), 1)
    all_columns = lax.all_gather(stick_column, "fft", axis=0, tiled=True)
    owners = all_columns.shape[0] // stick_count
    block_columns = (all_columns % slab_cells).reshape(owners, stick_count)
    block_hot = (
        block_columns[:, :, None] == jnp.arange(slab_cells, dtype=jnp.int32)[None, None, :]
    ).astype(jnp.bfloat16)

    def stick_work(one_band):
        plane_depth = one_band.shape[1]
        split_band = one_band.reshape(2, plane_depth, owners, stick_count)
        plane_grid = jnp.einsum(
            "pzds,dsc->pzdc", split_band, block_hot, preferred_element_type=jnp.float32
        ).astype(jnp.bfloat16)
        plane_grid = plane_grid.reshape(2, plane_depth, grid_size, grid_size)
        along_y = packed(apply_dft(plane_grid[0], plane_grid[1], forward, "zxy,yk->zxk"), 0)
        back_y = potential_work(along_y)
        back_split = back_y.reshape(2, plane_depth, owners, slab_cells)
        picked = jnp.einsum(
            "pzdc,dsc->pzds", back_split, block_hot, preferred_element_type=jnp.float32
        ).astype(jnp.bfloat16)
        return picked.reshape(2, plane_depth, owners * stick_count)

    finished = lax.map(
        stick_work, lax.all_to_all(along_z, "fft", split_axis=2, concat_axis=3, tiled=True)
    )
    stick_values = lax.all_to_all(finished, "fft", split_axis=3, concat_axis=2, tiled=True)
    picked_sticks = jnp.einsum(
        "bpzs,si->bpzi", stick_values, stick_hot, preferred_element_type=jnp.float32
    ).astype(jnp.bfloat16)
    cosine_cols = jnp.einsum("zk,ki->zi", inverse[0], plane_hot, preferred_element_type=jnp.float32)
    sine_cols = jnp.einsum("zk,ki->zi", inverse[1], plane_hot, preferred_element_type=jnp.float32)
    pick_real = picked_sticks[:, 0].astype(jnp.float32)
    pick_imag = picked_sticks[:, 1].astype(jnp.float32)
    wave_real = jnp.sum(pick_real * cosine_cols[None] - pick_imag * sine_cols[None], axis=1)
    wave_imag = jnp.sum(pick_real * sine_cols[None] + pick_imag * cosine_cols[None], axis=1)
    real_out = wave_real + kinetic * orbitals[:, 0].astype(jnp.float32)
    imag_out = wave_imag + kinetic * orbitals[:, 1].astype(jnp.float32)
    applied = jnp.stack([real_out, imag_out], axis=1).astype(jnp.bfloat16)
    return (applied, intersection)


PLANES = 4
PAIR = 2
LANES = 128
CHUNK = 4 * PLANES
EXTRA = 16


def phases(products, length):
    angle = (products % length).astype(np.float64) * (2.0 * np.pi / length)
    return np.cos(angle), np.sin(angle)


def as_bf16(array):
    return jnp.asarray(array, jnp.bfloat16)


def line_tables(length):
    cosine, sine = phases(np.outer(np.arange(length), np.arange(length)), length)

    def spread(table):
        rest = table[:, LANES:]
        return table[:, :LANES], np.concatenate([rest, rest], axis=1)

    tables = []
    for to_real, to_imag in ((cosine, sine), (-sine, cosine)):
        real_main, real_rest = spread(to_real)
        imag_main, imag_rest = spread(to_imag)
        tables.append(np.concatenate([real_main, imag_main, real_rest, imag_rest], axis=1))
    there = np.stack(tables)
    return as_bf16(there), as_bf16(there.transpose(0, 2, 1))


def half_tables(length):
    half = np.arange(length // 2)
    natural = np.arange(length).reshape(2, length // 16, 8)
    mixed = natural.transpose(1, 0, 2).reshape(-1)
    there, back = [], []
    for parity in (0, 1):
        cosine, sine = phases(np.outer(2 * half + parity, half), length)
        table = np.block([[cosine, -sine], [sine, cosine]])
        there.append(table[:, mixed])
        back.append(table.T)
    return as_bf16(np.stack(there + back))


def column_tables(length, slab):
    cosine, sine = phases(np.outer(np.arange(length), np.arange(length)), length)
    table = np.block([[cosine, -sine], [sine, cosine]])
    order = np.arange(2 * length).reshape(2, length // slab, slab // PLANES, PLANES)
    order = order.transpose(2, 1, 0, 3).reshape(-1)
    there = table[order]
    return as_bf16(there), as_bf16(there.T)


def pick_table(slab):
    lines = PLANES * PAIR
    table = np.zeros((CHUNK, lines * slab))
    for plane in range(PLANES):
        for band in range(PAIR):
            line = plane * PAIR + band
            for part in range(2):
                row = band * 2 * PLANES + part * PLANES + plane
                table[row, line * slab : (line + 1) * slab] = 1.0
    return as_bf16(table)


def whole_kernel(
    wave_ref,
    slot_ref,
    coord_ref,
    extra_ref,
    pot_ref,
    deep_ref,
    rise_ref,
    line_ref,
    turn_ref,
    half_ref,
    pick_ref,
    out_ref,
    extra_back_ref,
    full_ref,
    left_ref,
    right_ref,
    hot_ref,
    spread_ref,
    sent_ref,
    stick_ref,
    coords_ref,
    mask_ref,
    there_ref,
    again_ref,
    mixed_ref,
    heavy_ref,
    after_ref,
    kept_ref,
    stage_ref,
    back_ref,
    pot_sem,
    send_sem,
    recv_sem,
    home_send,
    home_recv,
    side_send,
    side_recv,
):
    slab, size, _ = pot_ref.shape
    owners = size // slab
    half_owners = owners // 2
    half = size // 2
    groups_pair = slab // PLANES
    blocks = wave_ref.shape[1]
    sticks = LANES
    lines = PLANES * PAIR
    pairs = wave_ref.shape[0] // (2 * PAIR)
    groups = pairs * groups_pair
    rest = size - LANES
    scale = 1.0 / (size * size)
    me = lax.axis_index("fft")
    others = [lax.rem(me + shift, owners) for shift in range(1, owners)]
    f32, bf16 = jnp.float32, jnp.bfloat16

    def dot(left, right):
        return jnp.dot(left, right, preferred_element_type=f32)

    def remote(src, dst, send, recv, place):
        return pltpu.make_async_remote_copy(
            src_ref=src,
            dst_ref=dst,
            send_sem=send,
            recv_sem=recv,
            device_id={"fft": others[place]},
            device_id_type=pl.DeviceIdType.MESH,
        )

    def coord_copy(place):
        return remote(
            coord_ref, coords_ref.at[me], side_send.at[0, place], side_recv.at[0, place], place
        )

    def extra_copy(place):
        return remote(
            extra_ref.at[others[place]],
            extra_back_ref.at[me],
            side_send.at[1, place],
            side_recv.at[1, place],
            place,
        )

    def there_copy(group, place):
        return remote(
            sent_ref.at[group, others[place]],
            stick_ref.at[group, me],
            send_sem.at[group, place],
            recv_sem.at[group, place],
            place,
        )

    def home_copy(group, place):
        return remote(
            stage_ref.at[group + 2, others[place]],
            back_ref.at[group, me],
            home_send.at[group, place],
            home_recv.at[group, place],
            place,
        )

    main_copy = pltpu.make_async_copy(pot_ref.at[:, :, :LANES], left_ref, pot_sem.at[0])
    rest_copy = pltpu.make_async_copy(pot_ref, full_ref, pot_sem.at[1])
    main_copy.start()
    rest_copy.start()

    barrier = pltpu.get_barrier_semaphore()
    for other in others:
        pl.semaphore_signal(
            barrier, inc=1, device_id={"fft": other}, device_id_type=pl.DeviceIdType.MESH
        )

    low_lane = lax.broadcasted_iota(jnp.int32, (1, LANES), 1) < rest
    level = lax.broadcasted_iota(jnp.int32, (half, LANES), 0)

    @pl.loop(0, blocks, unroll=4)
    def _(block):
        slot = slot_ref[pl.ds(block, 1), :]
        plane = lax.shift_right_logical(slot, 7)
        cell = jnp.where(plane >= half, sticks, 0) + jnp.bitwise_and(slot, sticks - 1)
        rows = lax.broadcasted_iota(jnp.int32, (2 * sticks, LANES), 0)
        place = pl.ds(pl.multiple_of(block * LANES, LANES), LANES)
        hot_ref[:, place] = jnp.where(cell == rows, 1.0, 0.0).astype(bf16)

    pl.semaphore_wait(barrier, owners - 1)
    for place in range(owners - 1):
        coord_copy(place).start()
    for place in range(owners - 1):
        extra_copy(place).start()
    coords_ref[me] = coord_ref[...]
    extra_back_ref[me] = extra_ref[me]

    def level_mask(block):
        plane = lax.shift_right_logical(slot_ref[pl.ds(block, 1), :], 7)
        return jnp.where(plane >= half, plane - half, plane) == level

    @pl.loop(0, pairs)
    def _(pair):
        @pl.loop(0, blocks, unroll=4)
        def _(block):
            chosen = level_mask(block)
            place = pl.ds(pl.multiple_of(block * LANES, LANES), LANES)
            for part in range(2 * PAIR):
                values = wave_ref[2 * PAIR * pair + part, pl.ds(block, 1), :]
                spread_ref[part * half : (part + 1) * half, place] = jnp.where(
                    chosen, values, 0.0
                ).astype(bf16)

        cells = lax.dot_general(
            spread_ref[...], hot_ref[...], (((1,), (1,)), ((), ())), preferred_element_type=f32
        )
        columns = []
        for band in range(PAIR):
            pieces = []
            for part in range(2):
                start = (2 * band + part) * half
                for side in range(2):
                    pieces.append(cells[start : start + half, side * LANES : (side + 1) * LANES])
            columns.append(jnp.concatenate(pieces, axis=0))
        columns = jnp.concatenate(columns, axis=1).astype(bf16)
        along = dot(deep_ref[...], columns).reshape(groups_pair * owners, 2 * PLANES, PAIR * LANES)
        chunks = jnp.concatenate([along[:, :, :LANES], along[:, :, LANES:]], axis=1)
        first = pair * groups_pair
        sent_ref[pl.ds(first, groups_pair)] = chunks.astype(bf16).reshape(
            groups_pair, owners, CHUNK, LANES
        )

        @pl.loop(0, groups_pair)
        def _(step):
            for place in range(owners - 1):
                there_copy(first + step, place).start()
            stick_ref[first + step, me] = sent_ref[first + step, me]

    main_copy.wait()
    rest_copy.wait()

    @pl.loop(0, slab)
    def _(plane):
        local = full_ref[plane, :, LANES:]
        right_ref[plane] = jnp.concatenate([local, local], axis=1)

    for place in range(owners - 1):
        coord_copy(place).wait()

    @pl.loop(0, owners)
    def _(owner):
        coords = coords_ref[owner]
        local = lax.broadcasted_iota(jnp.int32, (slab, sticks), 0).astype(f32)
        mask_ref[owner] = jnp.where(coords[0:1, :] == local, 1.0, 0.0)
        cells = lax.broadcasted_iota(jnp.int32, (size, sticks), 0).astype(f32)
        hot = jnp.where(coords[1:2, :] == cells, 1.0, 0.0).astype(bf16)
        for part in range(2):
            rows = lax.dot_general(
                hot, line_ref[part], (((0,), (0,)), ((), ())), preferred_element_type=f32
            )
            there_ref[owner, part * sticks : (part + 1) * sticks, :] = rows.astype(bf16)
            turned = dot(turn_ref[part], hot)
            again_ref[owner, :, part * sticks : (part + 1) * sticks] = turned.astype(bf16)

    def spread_lines(group):
        for low in range(half_owners):
            results = []
            for owner in (low, low + half_owners):
                values = stick_ref[group, owner].astype(f32)
                mask = mask_ref[owner]
                parts = []
                for part in range(2):
                    pieces = []
                    for plane in range(PLANES):
                        for band in range(PAIR):
                            row = band * 2 * PLANES + part * PLANES + plane
                            pieces.append(values[row : row + 1, :] * mask)
                    parts.append(jnp.concatenate(pieces, axis=0))
                left = jnp.concatenate(parts, axis=1).astype(bf16)
                results.append(dot(left, there_ref[owner]))
            for plane in range(PLANES):
                unit, side = plane // 2, plane % 2
                start = plane * PAIR * slab

                def pieces_of(result):
                    one = result[start : start + slab]
                    two = result[start + slab : start + 2 * slab]
                    found = []
                    for half_lines in (one, two):
                        found.append((half_lines[:, :LANES], half_lines[:, LANES : 2 * LANES]))
                    both = []
                    for offset in (2 * LANES, 3 * LANES):
                        both.append(
                            jnp.where(
                                low_lane,
                                one[:, offset : offset + LANES],
                                two[:, offset : offset + LANES],
                            )
                        )
                    found.append(tuple(both))
                    return found

                near, far = pieces_of(results[0]), pieces_of(results[1])
                offsets = (2 * side * LANES, (2 * side + 1) * LANES, (4 + side) * LANES)
                for (near_re, near_im), (far_re, far_im), offset in zip(near, far, offsets):
                    for parity in range(2):
                        if parity == 0:
                            real, imag = near_re + far_re, near_im + far_im
                        else:
                            real, imag = near_re - far_re, near_im - far_im
                        tile = jnp.concatenate(
                            [real.reshape(-1, 8, LANES), imag.reshape(-1, 8, LANES)], axis=1
                        )
                        mixed_ref[
                            unit,
                            parity,
                            slice(2 * slab * low, 2 * slab * (low + 1)),
                            offset : offset + LANES,
                        ] = tile.reshape(2 * slab, LANES).astype(bf16)

    def forward_lines(group, unit):
        first = lax.rem(group, groups_pair) * PLANES
        if True:
            for parity in range(2):
                picks = pl.ds(parity, half, 2)

                for tile in range(3):
                    result = dot(
                        half_ref[parity],
                        mixed_ref[unit, parity, :, 2 * LANES * tile : 2 * LANES * (tile + 1)],
                    )
                    if tile < 2:
                        local = left_ref[first + 2 * unit + tile, picks, :]
                        local = jnp.concatenate([local, local], axis=1)
                    else:
                        one = right_ref[first + 2 * unit, picks, :]
                        two = right_ref[first + 2 * unit + 1, picks, :]
                        local = jnp.concatenate([one, two], axis=1)
                    heavy_ref[unit, parity, tile, :half] = (result[:half] * local).astype(bf16)
                    heavy_ref[unit, parity, tile, half:] = (result[half:] * local).astype(bf16)

    def backward_lines(unit):
        if True:
            for tile in range(3):
                even = dot(half_ref[2], heavy_ref[unit, 0, tile])
                odd = dot(half_ref[3], heavy_ref[unit, 1, tile])
                for side, values in enumerate((even + odd, even - odd)):
                    for low in range(half_owners):
                        owner = low + side * half_owners
                        for part in range(2):
                            start = part * half + low * slab
                            found = values[start : start + slab]
                            one, two = found[:, :LANES], found[:, LANES:]
                            if tile < 2:
                                rows = pl.ds(
                                    pl.multiple_of((2 * unit + tile) * 2 * slab, 2 * slab), 2 * slab
                                )
                                after_ref[owner, rows, part * LANES : (part + 1) * LANES] = (
                                    jnp.concatenate([one, two], axis=0).astype(bf16)
                                )
                            else:
                                for place, both in enumerate((one, two)):
                                    plane = 2 * unit + place
                                    rows = pl.ds(
                                        pl.multiple_of(plane * 2 * slab, 2 * slab), 2 * slab
                                    )
                                    after_ref[
                                        owner, rows, (2 + part) * LANES : (3 + part) * LANES
                                    ] = jnp.concatenate(
                                        [
                                            jnp.where(low_lane, both, 0.0),
                                            jnp.where(low_lane, 0.0, both),
                                        ],
                                        axis=0,
                                    ).astype(bf16)

    part_row = lax.broadcasted_iota(jnp.int32, (CHUNK, LANES), 0)
    part_row = jnp.bitwise_and(part_row, PLANES) == 0

    def weighed_lines():
        for owner in range(owners):
            result = dot(after_ref[owner], again_ref[owner])
            mask = mask_ref[owner] * scale
            mask = jnp.concatenate([mask, mask], axis=1)[None]
            kept = (result.reshape(lines, slab, 2 * LANES) * mask).reshape(lines * slab, 2 * LANES)
            kept_ref[owner] = kept.astype(bf16)

    def picked_lines(place):
        for owner in range(owners):
            found = dot(pick_ref[...], kept_ref[owner])
            stage_ref[place, owner] = jnp.where(
                part_row, found[:, :LANES], found[:, LANES:]
            ).astype(bf16)

    def wait_group(group):
        for place in range(owners - 1):
            there_copy(group, place).wait()

    def send_home(group):
        for place in range(owners - 1):
            home_copy(group, place).start()
        back_ref[group, me] = stage_ref[group + 2, me]

    wait_group(0)
    spread_lines(0)

    @pl.loop(0, groups)
    def _(group):
        @pl.when(group < groups - 1)
        def _():
            wait_group(group + 1)

        forward_lines(group, 0)
        forward_lines(group, 1)
        picked_lines(group)
        weighed_lines()
        backward_lines(0)
        backward_lines(1)
        spread_lines(lax.rem(group + 1, groups))

        @pl.when(group > 1)
        def _():
            send_home(group - 2)

    picked_lines(groups)
    weighed_lines()
    send_home(groups - 2)
    picked_lines(groups + 1)
    send_home(groups - 1)

    for place in range(owners - 1):
        extra_copy(place).wait()

    @pl.loop(0, pairs)
    def _(pair):
        first = pair * groups_pair

        @pl.loop(0, groups_pair)
        def _(step):
            for place in range(owners - 1):
                home_copy(first + step, place).wait()

        chunks = back_ref[pl.ds(first, groups_pair)].reshape(groups_pair * owners, CHUNK, LANES)
        chunks = chunks.astype(f32)
        columns = []
        for band in range(PAIR):
            rows = chunks[:, band * 2 * PLANES : (band + 1) * 2 * PLANES]
            columns.append(rows.reshape(2 * size, LANES))
        columns = jnp.concatenate(columns, axis=1).astype(bf16)
        risen = (dot(rise_ref[...], columns) * (1.0 / size)).astype(bf16)
        pieces = []
        for band in range(PAIR):
            for part in range(2):
                both = []
                for side in range(2):
                    start = part * size + side * half
                    both.append(risen[start : start + half, band * LANES : (band + 1) * LANES])
                pieces.append(jnp.concatenate(both, axis=1))
        spread_ref[:, : 2 * LANES] = jnp.concatenate(pieces, axis=0)

        @pl.loop(0, blocks // 2, unroll=2)
        def _(step):
            place = pl.ds(pl.multiple_of(step * 2 * LANES, LANES), 2 * LANES)
            values = dot(spread_ref[:, : 2 * LANES], hot_ref[:, place])
            for side in range(2):
                block = 2 * step + side
                chosen = level_mask(block)
                for part in range(2 * PAIR):
                    mine = values[part * half : (part + 1) * half, side * LANES : (side + 1) * LANES]
                    out_ref[2 * PAIR * pair + part, pl.ds(block, 1), :] = jnp.sum(
                        jnp.where(chosen, mine, 0.0), axis=0, keepdims=True
                    )


def whole_work(waves, slots, coords, extra, potential):
    slab, size, _ = potential.shape
    owners = size // slab
    groups_pair = slab // PLANES
    parts, blocks, _ = waves.shape
    pairs = parts // (2 * PAIR)
    groups = pairs * groups_pair
    half = size // 2
    lines = PLANES * PAIR
    deep, rise = column_tables(size, slab)
    line, turn = line_tables(size)
    halves = half_tables(size)
    pick = pick_table(slab)
    in_vmem = pl.BlockSpec(memory_space=pltpu.VMEM)
    anywhere = pl.BlockSpec(memory_space=pl.ANY)
    bf16, f32 = jnp.bfloat16, jnp.float32
    dma = pltpu.SemaphoreType.DMA
    return pl.pallas_call(
        whole_kernel,
        out_shape=(
            jax.ShapeDtypeStruct(waves.shape, f32),
            jax.ShapeDtypeStruct(extra.shape, bf16),
        ),
        in_specs=[in_vmem] * 4 + [anywhere] + [in_vmem] * 6,
        out_specs=(in_vmem, in_vmem),
        scratch_shapes=[
            pltpu.VMEM((slab, size, size), f32),
            pltpu.VMEM((slab, size, LANES), f32),
            pltpu.VMEM((slab, size, LANES), f32),
            pltpu.VMEM((2 * LANES, blocks * LANES), bf16),
            pltpu.VMEM((2 * PAIR * half, blocks * LANES), bf16),
            pltpu.VMEM((groups, owners, CHUNK, LANES), bf16),
            pltpu.VMEM((groups, owners, CHUNK, LANES), bf16),
            pltpu.VMEM((owners, 8, LANES), f32),
            pltpu.VMEM((owners, slab, LANES), f32),
            pltpu.VMEM((owners, 2 * LANES, 4 * LANES), bf16),
            pltpu.VMEM((owners, 4 * LANES, 2 * LANES), bf16),
            pltpu.VMEM((PLANES // 2, 2, size, 6 * LANES), bf16),
            pltpu.VMEM((PLANES // 2, 2, 3, size, 2 * LANES), bf16),
            pltpu.VMEM((owners, lines * slab, 4 * LANES), bf16),
            pltpu.VMEM((owners, lines * slab, 2 * LANES), bf16),
            pltpu.VMEM((groups + 2, owners, CHUNK, LANES), bf16),
            pltpu.VMEM((groups, owners, CHUNK, LANES), bf16),
            dma((2,)),
            dma((groups, owners - 1)),
            dma((groups, owners - 1)),
            dma((groups, owners - 1)),
            dma((groups, owners - 1)),
            dma((2, owners - 1)),
            dma((2, owners - 1)),
        ],
        compiler_params=pltpu.CompilerParams(
            collective_id=0, has_side_effects=True, vmem_limit_bytes=56 * 1024 * 1024
        ),
        cost_estimate=pl.CostEstimate(
            flops=40 * 10**9, bytes_accessed=8 * 10**6, transcendentals=0
        ),
    )(waves, slots, coords, extra, potential, deep, rise, line, turn, halves, pick)


def gathered_bands(array, mesh_bands):
    here = lax.axis_index("band")
    blocks = [array]
    for shift in range(1, mesh_bands):
        pairs = [((src + shift) % mesh_bands, src) for src in range(mesh_bands)]
        blocks.append(lax.ppermute(array, "band", pairs))
    return blocks, here


def overlaps(subspace, previous, mesh_bands, owners):
    blocks, here = gathered_bands(subspace, mesh_bands)
    prev_real, prev_imag = previous[:, 0], previous[:, 1]
    right = jnp.concatenate(
        [
            jnp.concatenate([prev_real, prev_imag], axis=1),
            jnp.concatenate([prev_imag, -prev_real], axis=1),
        ],
        axis=0,
    )
    partials = []
    for block in blocks:
        partials.append(
            jnp.einsum(
                "jg,ig->ji",
                block.reshape(block.shape[0], -1),
                right,
                preferred_element_type=jnp.float32,
            )
        )
    twice = jnp.concatenate(partials + partials, axis=0)
    count = twice.shape[0] // 2
    start = (count - here * subspace.shape[0]) % count
    ordered = lax.dynamic_slice_in_dim(twice, start, count, axis=0)
    split = ordered.reshape(owners, count // owners, 2, previous.shape[0])
    return split.transpose(0, 2, 1, 3)


def fast_device(mesh_bands, orbitals, sphere_slot, stick_column, potential, subspace, previous):
    slab_depth, grid_size, _ = potential.shape
    stick_count = stick_column.shape[0]
    owners = grid_size // slab_depth
    bands = orbitals.shape[0]
    plane_index = sphere_slot // stick_count
    stick_index = sphere_slot % stick_count
    stick_hot = one_hot_rows(stick_index, stick_count)
    stick_x = stick_column // grid_size
    stick_y = stick_column % grid_size
    stick_coords = jnp.stack([stick_x, stick_y]).astype(jnp.bfloat16)
    wave_coords = jnp.dot(stick_coords, stick_hot, preferred_element_type=jnp.float32)
    freq_z = frequency(plane_index, grid_size)
    freq_x = frequency(wave_coords[0].astype(jnp.int32), grid_size)
    freq_y = frequency(wave_coords[1].astype(jnp.int32), grid_size)
    kinetic = (freq_z * freq_z + freq_x * freq_x + freq_y * freq_y) * (
        2.0 / (grid_size * grid_size)
    )
    local_x = stick_x - lax.axis_index("fft") * slab_depth
    coords = jnp.stack([local_x, stick_y]).astype(jnp.float32)
    coords = jnp.pad(coords, ((0, 8 - 2), (0, 0)))
    split = overlaps(subspace, previous, mesh_bands, owners)
    flat = split.reshape(owners, 1, -1)
    high = lax.reduce_precision(flat, 8, 7)
    low = lax.reduce_precision(flat - high, 8, 7)
    both = jnp.concatenate([high, low], axis=2).astype(jnp.bfloat16)
    width = both.shape[2]
    lanes = -(-width // stick_count) * stick_count
    both = jnp.pad(both, ((0, 0), (0, 0), (0, lanes - width)))
    both = both.reshape(owners, -1, stick_count)
    both = jnp.pad(both, ((0, 0), (0, EXTRA - both.shape[1]), (0, 0)))
    waves = orbitals.astype(jnp.float32).reshape(2 * bands, -1, LANES)
    slots = sphere_slot.reshape(-1, LANES)
    found, returned = whole_work(waves, slots, coords, both, potential)
    sums = returned.reshape(owners, -1)[:, :width].astype(jnp.float32)
    sums = jnp.sum(sums, axis=0)
    intersection = (sums[: width // 2] + sums[width // 2 :]).reshape(split.shape[1:])
    found = found.reshape(orbitals.shape)
    applied = (found + kinetic * orbitals.astype(jnp.float32)).astype(jnp.bfloat16)
    return (applied, intersection)


def per_device(mesh_bands, *arrays):
    orbitals, slots, sticks, potential, _, _ = arrays
    slab, size, _ = potential.shape
    owners = size // slab
    fits = slab % 8 == 0 and owners % 2 == 0 and owners * slab == size
    fits = fits and 2 * size == 3 * LANES and sticks.shape[0] == LANES
    fits = fits and orbitals.shape[0] % PAIR == 0 and slots.shape[0] % (2 * LANES) == 0
    if fits:
        return fast_device(mesh_bands, *arrays)
    return general_device(*arrays)


def solution(mesh):
    return jax.shard_map(
        functools.partial(per_device, mesh.shape["band"]),
        mesh=mesh,
        in_specs=(
            P("band", None, "fft"),
            P("fft"),
            P("fft"),
            P("fft", None, None),
            P("band", None, "fft"),
            P("band", None, "fft"),
        ),
        out_specs=(P("band", None, "fft"), P(None, "fft", "band")),
        check_vma=False,
    )
```

time: 88.9 us -> 72.4 us (0.81)
  Pallas kernels: 62.2 us -> 51.4 us
  matrix products: 10.5 us -> 1.25 us
  waiting for transfers between devices: 0.01 us -> 3.44 us
  other arithmetic: 2.78 us -> 3.75 us
    pallas_call x1, Pallas kernels: 62.2 us -> 51.4 us  [whole_work(): pl.pallas_call(whole_kernel, out_shape=(jax.ShapeDtypeStruct(waves.shape,...]
    dot_general x4 -> x0, matrix products: 7.78 us -> none  [the longest x1 4.08 us: fast_device(): jnp.einsum('pzbs,si->pzbi', columns, stick_hot, preferred_element_type=jn...]
    ppermute x3, waiting for transfers between devices: 0.01 us -> 3.44 us  [gathered_bands(): blocks.append(lax.ppermute(array, 'band', pairs))]
    slice x3 -> x0, local copies, waits for them, and re-layouts: 1.72 us -> none  [the longest x1 1.66 us: fast_device(): real_out = wave_real + kinetic * orbitals[:, 0].astype(jnp.float32)]
    dot_general x4, matrix products: 2.33 us -> 0.82 us  [overlaps(): jnp.einsum('jg,ig->ji', block.reshape(block.shape[0], -1), right, preferr...]
    reshape x1 -> x2, local copies, waits for them, and re-layouts: 0.28 us -> 1.67 us  [the longest x1 0.97 us: fast_device(): found = found.reshape(orbitals.shape)]
    another operation x6 -> x1, other arithmetic: 1.28 us -> 0.01 us  [fast_device(): coords = jnp.stack([local_x, stick_y]).astype(jnp.float32)]
    unnamed x27 -> x9, local copies, waits for them, and re-layouts: 3.07 us -> 3.07 us
  transfers between devices with their start and end apart: 3 -> 3, of which waited for: 0 -> 1; matrix products, arithmetic and copies ran while one was open for 15% -> 10% of each run, Pallas kernels for 0% -> 0%
where the time goes in v1:
time: 72.4 us; the launch traced here: 72 us
  Pallas kernels  51.4 us (71%)
  local copies, waits for them, and re-layouts  6.85 us (9%)
  starting transfers between devices  4.48 us (6%)
  other arithmetic  3.75 us (5%)
  waiting for transfers between devices  3.44 us (5%)
  matrix products  1.25 us (2%)
  between operations  0.75 us (1%)
    pallas_call x1, Pallas kernels, whole_work(): pl.pallas_call(whole_kernel, out_shape=(jax.ShapeDtypeStruct(waves.shape,...  51.4 us
    ppermute x3, starting transfers between devices, gathered_bands(): blocks.append(lax.ppermute(array, 'band', pairs))  4.48 us
    ppermute x3, waiting for transfers between devices, gathered_bands(): blocks.append(lax.ppermute(array, 'band', pairs))  3.44 us
    unnamed x9, local copies, waits for them, and re-layouts  3.07 us
  transfers between devices with their start and end apart: 3, of which 1 were waited for; matrix products, arithmetic and copies ran while one was open for 10% of the time, Pallas kernels for 0%

profile of v1, /device:TPU:0, one launch (start us, length us, event | category | flops | bytes accessed | tf_op | source)
XLA Modules:
  0.0 72.0 jit_solution(14356084196251603893)
XLA Ops:
  0.6 0.0 copy-start
  0.6 0.5 collective-permute-start.2
  1.2 2.6 %collective-permute-start.1 = (bf16[16,2,4096]{2,1,0:T(2,128)(2,1)}, bf16[16,2,4096]{2,1,0:T(2,128)(2,1)S(1)}, u32[]{:S(2)}, u32[]{:S(2)}) collective-permute-start(bf16[16,2,4096]{2,1,0:T(2,128)(2,1)} %param.16), channel_id=1, source_target_pairs={{16,0},{24,8},{0,16},{8,24},{17,1},{25,9},{1,17},{9,25},{18,2},{26... | collective-permute-start | bytes 786440 | tf_op jit(solution)/shard_map/ppermute | solution.py:670
  3.7 1.4 %collective-permute-start = (bf16[16,2,4096]{2,1,0:T(2,128)(2,1)}, bf16[16,2,4096]{2,1,0:T(2,128)(2,1)S(1)}, u32[]{:S(2)}, u32[]{:S(2)}) collective-permute-start(bf16[16,2,4096]{2,1,0:T(2,128)(2,1)} %param.16), channel_id=1, source_target_pairs={{8,0},{16,8},{24,16},{0,24},{9,1},{17,9},{25,17},{1,25},{10,2},{18... | collective-permute-start | bytes 786440 | tf_op jit(solution)/shard_map/ppermute | solution.py:670
  5.1 1.0 %fusion.27 = (bf16[4,1,4096]{2,1,0:T(2,128)(2,1)S(1)}, bf16[4,1,4096]{2,1,0:T(2,128)(2,1)S(1)}) fusion(bf16[4,2,4096]{2,1,0:T(2,128)(2,1)} %param.17), kind=kLoop, calls=%fused_computation.59 | loop fusion | bytes 131072 | tf_op jit(solution)/shard_map/slice | solution.py:676
  6.2 0.1 fusion.26
  6.3 1.1 %copy.39 = bf16[2,8,2,4096]{3,1,2,0:T(8,128)(2,1)S(1)} copy(bf16[2,8,2,4096]{3,2,1,0:T(2,128)(2,1)} %bitcast.49) | data formatting | bytes 524288
  7.4 0.7 convert_bitcast_fusion
  8.1 0.7 %add_select_fusion = s32[4096]{0:T(1024)S(1)} fusion(s32[4096]{0:T(1024)} %param.13), kind=kLoop, calls=%fused_computation.19 | loop fusion | flops 45056 | bytes 32768 | tf_op jit(solution)/shard_map/jit(remainder)/select_n | solution.py:708
  8.8 0.4 fusion
  9.3 0.7 %fusion.9 = f32[4096]{0:T(1024)S(1)} fusion(s32[4096]{0:T(1024)S(1)} %bitcast.61, s32[4096]{0:T(1024)S(1)} %bitcast.60, s32[4096]{0:T(1024)} %param.13), kind=kLoop, calls=%fused_computation.28 | loop fusion | flops 135168 | bytes 65536 | tf_op jit(solution)/shard_map/mul | solution.py:717
  10.0 0.2 convolution_bitcast_fusion.3
  10.2 0.0 copy-done
  10.2 0.7 reshape.101.wave_ref
  10.9 0.6 pad.8.coord_ref
  11.5 0.0 collective-permute-done.2
  11.5 0.1 copy.42
  11.7 0.2 convolution_bitcast_fusion
  11.9 0.0 collective-permute-done.1
  11.9 0.2 copy.41
  12.1 0.2 convolution_bitcast_fusion.1
  12.3 3.4 %collective-permute-done = bf16[16,2,4096]{2,1,0:T(2,128)(2,1)S(1)} collective-permute-done((bf16[16,2,4096]{2,1,0:T(2,128)(2,1)}, bf16[16,2,4096]{2,1,0:T(2,128)(2,1)S(1)}, u32[]{:S(2)}, u32[]{:S(2)}) %collective-permute-start) | collective-permute-done | bytes 262176 | tf_op jit(solution)/shard_map/ppermute | solution.py:670
  15.7 0.1 copy.40
  15.9 0.2 convolution_bitcast_fusion.2
  16.1 0.1 concatenate.31
  16.2 0.1 constant_dynamic-slice_fusion
  16.2 0.1 reshape.107
  16.3 0.1 copy.31
  16.4 0.1 copy.32
  16.5 0.7 fusion.4.extra_ref
  17.2 51.4 %shard_map.131 = (f32[8,32,128]{2,1,0:T(8,128)}, bf16[8,16,128]{2,1,0:T(8,128)(2,1)}) custom-call(f32[8,32,128]{2,1,0:T(8,128)} %reshape.101.wave_ref, s32[32,128]{1,0:T(8,128)} %bitcast.59, f32[8,128]{1,0:T(8,128)} %pad.8.coord_ref, bf16[8,16,128]{2,1,0:T(8,128)(2,1)} %fusion.4.extra_ref, f32[24,192,192]{2,1,0:T(8,128)} %pot_ref.1, ...), custom_call_target="tpu_custom_call" | custom-call | flops 40000000000 | bytes 8000000 | tf_op jit(solution)/shard_map/pallas_call | solution.py:622
  68.7 1.0 %reshape.109 = f32[4,2,4096]{2,1,0:T(2,128)S(1)} reshape(f32[8,32,128]{2,1,0:T(8,128)} %get-tuple-element.4) | data formatting | bytes 262144 | tf_op jit(solution)/shard_map/reshape | solution.py:739
  69.6 0.8 %copy.48 = bf16[1,8,16,128]{3,1,2,0:T(8,128)(2,1)S(1)} copy(bf16[1,8,16,128]{3,2,1,0:T(8,128)(2,1)} %bitcast.67) | data formatting | bytes 65536
  70.4 0.1 slice_add_fusion
  70.5 0.1 add.52
  70.6 0.7 copy.36
  71.3 0.7 add_convert_fusion
  (8 shorter events, 0.1 us)
Async XLA Ops:
  0.6 9.6 %copy-start = (bf16[4,2,4096]{2,1,0:T(2,128)(2,1)S(1)}, bf16[4,2,4096]{2,1,0:T(2,128)(2,1)}, u32[]{:S(2)}) copy-start(bf16[4,2,4096]{2,1,0:T(2,128)(2,1)} %param.12) | copy-start | bytes 196612
  0.6 10.9 %collective-permute-start.2 = (bf16[16,2,4096]{2,1,0:T(2,128)(2,1)}, bf16[16,2,4096]{2,1,0:T(2,128)(2,1)S(1)}, u32[]{:S(2)}, u32[]{:S(2)}) collective-permute-start(bf16[16,2,4096]{2,1,0:T(2,128)(2,1)} %param.16), channel_id=1, source_target_pairs={{24,0},{0,8},{8,16},{16,24},{25,1},{1,9},{9,17},{17,25},{26,2},{2,... | collective-permute-start | bytes 786440 | tf_op jit(solution)/shard_map/ppermute | solution.py:670
  1.2 10.7 %collective-permute-start.1 = (bf16[16,2,4096]{2,1,0:T(2,128)(2,1)}, bf16[16,2,4096]{2,1,0:T(2,128)(2,1)S(1)}, u32[]{:S(2)}, u32[]{:S(2)}) collective-permute-start(bf16[16,2,4096]{2,1,0:T(2,128)(2,1)} %param.16), channel_id=1, source_target_pairs={{16,0},{24,8},{0,16},{8,24},{17,1},{25,9},{1,17},{9,25},{18,2},{26... | collective-permute-start | bytes 786440 | tf_op jit(solution)/shard_map/ppermute | solution.py:670
  3.7 12.0 %collective-permute-start = (bf16[16,2,4096]{2,1,0:T(2,128)(2,1)}, bf16[16,2,4096]{2,1,0:T(2,128)(2,1)S(1)}, u32[]{:S(2)}, u32[]{:S(2)}) collective-permute-start(bf16[16,2,4096]{2,1,0:T(2,128)(2,1)} %param.16), channel_id=1, source_target_pairs={{8,0},{16,8},{24,16},{0,24},{9,1},{17,9},{25,17},{1,25},{10,2},{18... | collective-permute-start | bytes 786440 | tf_op jit(solution)/shard_map/ppermute | solution.py:670

commit v2 on v1

--- a/solution.py
+++ b/solution.py
@@ -195,26 +195,38 @@
 
 
 def whole_kernel(
-    wave_ref,
+    mesh_bands,
+    orbital_ref,
     slot_ref,
-    coord_ref,
-    extra_ref,
+    column_ref,
+    previous_ref,
+    subspace_hbm,
     pot_ref,
+    deep_hbm,
+    rise_hbm,
+    line_hbm,
+    turn_hbm,
+    half_hbm,
+    pick_ref,
+    applied_ref,
+    inter_ref,
+    subspace_ref,
     deep_ref,
     rise_ref,
     line_ref,
     turn_ref,
     half_ref,
-    pick_ref,
-    out_ref,
-    extra_back_ref,
     full_ref,
     left_ref,
     right_ref,
+    wave_ref,
+    found_ref,
+    kinetic_ref,
     hot_ref,
-    spread_ref,
+    gather_ref,
     sent_ref,
     stick_ref,
+    coord_ref,
     coords_ref,
     mask_ref,
     there_ref,
@@ -225,55 +237,92 @@
     kept_ref,
     stage_ref,
     back_ref,
-    pot_sem,
+    every_ref,
+    right_side_ref,
+    share_ref,
+    shares_ref,
+    load_sem,
     send_sem,
     recv_sem,
     home_send,
     home_recv,
-    side_send,
-    side_recv,
+    coord_send,
+    coord_recv,
+    band_send,
+    band_recv,
+    share_send,
+    share_recv,
 ):
     slab, size, _ = pot_ref.shape
     owners = size // slab
     half_owners = owners // 2
     half = size // 2
     groups_pair = slab // PLANES
-    blocks = wave_ref.shape[1]
+    waves = slot_ref.shape[1]
+    blocks = waves // LANES
     sticks = LANES
     lines = PLANES * PAIR
-    pairs = wave_ref.shape[0] // (2 * PAIR)
+    bands = orbital_ref.shape[0]
+    pairs = bands // PAIR
     groups = pairs * groups_pair
     rest = size - LANES
     scale = 1.0 / (size * size)
+    mine = subspace_ref.shape[0]
+    share = share_ref.shape[1]
+    shares = mine // share
     me = lax.axis_index("fft")
+    band_me = lax.axis_index("band")
+    every_band = [lax.rem(band_me + shift, mesh_bands) for shift in range(mesh_bands)]
     others = [lax.rem(me + shift, owners) for shift in range(1, owners)]
     f32, bf16 = jnp.float32, jnp.bfloat16
 
     def dot(left, right):
         return jnp.dot(left, right, preferred_element_type=f32)
 
-    def remote(src, dst, send, recv, place):
+    def remote(src, dst, send, recv, target):
         return pltpu.make_async_remote_copy(
             src_ref=src,
             dst_ref=dst,
             send_sem=send,
             recv_sem=recv,
-            device_id={"fft": others[place]},
+            device_id=target,
             device_id_type=pl.DeviceIdType.MESH,
         )
 
     def coord_copy(place):
         return remote(
-            coord_ref, coords_ref.at[me], side_send.at[0, place], side_recv.at[0, place], place
+            coord_ref,
+            coords_ref.at[me],
+            coord_send.at[place],
+            coord_recv.at[place],
+            {"fft": others[place]},
         )
 
-    def extra_copy(place):
+    def band_copy(place):
         return remote(
-            extra_ref.at[others[place]],
-            extra_back_ref.at[me],
-            side_send.at[1, place],
-            side_recv.at[1, place],
-            place,
+            previous_ref,
+            every_ref.at[band_me],
+            band_send.at[place],
+            band_recv.at[place],
+            {"band": every_band[place + 1]},
+        )
+
+    def share_copy(block, place):
+        return remote(
+            share_ref.at[block],
+            shares_ref.at[me],
+            share_send.at[block, place],
+            share_recv.at[me],
+            {"band": every_band[place], "fft": shares * band_me + block},
+        )
+
+    def share_arrival(source):
+        return remote(
+            share_ref.at[0],
+            shares_ref.at[source],
+            share_send.at[0, 0],
+            share_recv.at[source],
+            {"fft": others[0]},
         )
 
     def there_copy(group, place):
@@ -282,7 +331,7 @@
             stick_ref.at[group, me],
             send_sem.at[group, place],
             recv_sem.at[group, place],
-            place,
+            {"fft": others[place]},
         )
 
     def home_copy(group, place):
@@ -291,59 +340,93 @@
             back_ref.at[group, me],
             home_send.at[group, place],
             home_recv.at[group, place],
-            place,
+            {"fft": others[place]},
         )
 
-    main_copy = pltpu.make_async_copy(pot_ref.at[:, :, :LANES], left_ref, pot_sem.at[0])
-    rest_copy = pltpu.make_async_copy(pot_ref, full_ref, pot_sem.at[1])
-    main_copy.start()
-    rest_copy.start()
+    loads = []
+    for place, (src, dst) in enumerate(
+        (
+            (deep_hbm, deep_ref),
+            (line_hbm, line_ref),
+            (turn_hbm, turn_ref),
+            (subspace_hbm, subspace_ref),
+            (pot_ref, full_ref),
+            (pot_ref.at[:, :, :LANES], left_ref),
+            (half_hbm, half_ref),
+            (rise_hbm, rise_ref),
+        )
+    ):
+        loads.append(pltpu.make_async_copy(src, dst, load_sem.at[place]))
+        loads[-1].start()
 
     barrier = pltpu.get_barrier_semaphore()
-    for other in others:
-        pl.semaphore_signal(
-            barrier, inc=1, device_id={"fft": other}, device_id_type=pl.DeviceIdType.MESH
-        )
+    for place in range(mesh_bands):
+        for other in [me] + others:
+            if place or other is not me:
+                pl.semaphore_signal(
+                    barrier,
+                    inc=1,
+                    device_id={"band": every_band[place], "fft": other},
+                    device_id_type=pl.DeviceIdType.MESH,
+                )
 
     low_lane = lax.broadcasted_iota(jnp.int32, (1, LANES), 1) < rest
     level = lax.broadcasted_iota(jnp.int32, (half, LANES), 0)
+    wave_ref[...] = orbital_ref[...].reshape(2 * bands, waves).astype(f32)
+
+    column = column_ref[...]
+    grid_x = jnp.floor((column.astype(f32) + 0.5) * (1.0 / size))
+    grid_y = column.astype(f32) - grid_x * size
+    coord_row = lax.broadcasted_iota(jnp.int32, (8, LANES), 0)
+    first_x = lax.convert_element_type(me * slab, f32)
+    coord_ref[...] = jnp.where(coord_row == 0, grid_x - first_x, jnp.where(coord_row == 1, grid_y, 0.0))
+
+    def lanes_of(block, count=1):
+        return pl.ds(pl.multiple_of(block * LANES, LANES), count * LANES)
+
+    def plane_of(block):
+        return lax.shift_right_logical(slot_ref[:, lanes_of(block)], 7)
 
     @pl.loop(0, blocks, unroll=4)
     def _(block):
-        slot = slot_ref[pl.ds(block, 1), :]
-        plane = lax.shift_right_logical(slot, 7)
-        cell = jnp.where(plane >= half, sticks, 0) + jnp.bitwise_and(slot, sticks - 1)
+        slot = slot_ref[:, lanes_of(block)]
+        cell = jnp.where(plane_of(block) >= half, sticks, 0) + jnp.bitwise_and(slot, sticks - 1)
         rows = lax.broadcasted_iota(jnp.int32, (2 * sticks, LANES), 0)
-        place = pl.ds(pl.multiple_of(block * LANES, LANES), LANES)
-        hot_ref[:, place] = jnp.where(cell == rows, 1.0, 0.0).astype(bf16)
-
-    pl.semaphore_wait(barrier, owners - 1)
+        hot_ref[:, lanes_of(block)] = jnp.where(cell == rows, 1.0, 0.0).astype(bf16)
+
+    pl.semaphore_wait(barrier, mesh_bands * owners - 1)
     for place in range(owners - 1):
         coord_copy(place).start()
-    for place in range(owners - 1):
-        extra_copy(place).start()
+    for place in range(mesh_bands - 1):
+        band_copy(place).start()
     coords_ref[me] = coord_ref[...]
-    extra_back_ref[me] = extra_ref[me]
+    every_ref[band_me] = previous_ref[...]
 
     def level_mask(block):
-        plane = lax.shift_right_logical(slot_ref[pl.ds(block, 1), :], 7)
+        plane = plane_of(block)
         return jnp.where(plane >= half, plane - half, plane) == level
 
-    @pl.loop(0, pairs)
-    def _(pair):
-        @pl.loop(0, blocks, unroll=4)
-        def _(block):
-            chosen = level_mask(block)
-            place = pl.ds(pl.multiple_of(block * LANES, LANES), LANES)
-            for part in range(2 * PAIR):
-                values = wave_ref[2 * PAIR * pair + part, pl.ds(block, 1), :]
-                spread_ref[part * half : (part + 1) * half, place] = jnp.where(
-                    chosen, values, 0.0
-                ).astype(bf16)
-
-        cells = lax.dot_general(
-            spread_ref[...], hot_ref[...], (((1,), (1,)), ((), ())), preferred_element_type=f32
-        )
+    def scatter_waves(pair):
+        cells = None
+        for block in range(0, blocks, 2):
+            pieces = []
+            for step in range(2):
+                chosen = level_mask(block + step)
+                values = wave_ref[
+                    2 * PAIR * pair : 2 * PAIR * (pair + 1), lanes_of(block + step)
+                ]
+                rows = []
+                for part in range(2 * PAIR):
+                    rows.append(jnp.where(chosen, values[part : part + 1], 0.0))
+                pieces.append(jnp.concatenate(rows, axis=0))
+            left = jnp.concatenate(pieces, axis=1).astype(bf16)
+            term = lax.dot_general(
+                left,
+                hot_ref[:, lanes_of(block, 2)],
+                (((1,), (1,)), ((), ())),
+                preferred_element_type=f32,
+            )
+            cells = term if cells is None else cells + term
         columns = []
         for band in range(PAIR):
             pieces = []
@@ -353,10 +436,12 @@
                     pieces.append(cells[start : start + half, side * LANES : (side + 1) * LANES])
             columns.append(jnp.concatenate(pieces, axis=0))
         columns = jnp.concatenate(columns, axis=1).astype(bf16)
+        if pair == 0:
+            loads[0].wait()
         along = dot(deep_ref[...], columns).reshape(groups_pair * owners, 2 * PLANES, PAIR * LANES)
         chunks = jnp.concatenate([along[:, :, :LANES], along[:, :, LANES:]], axis=1)
         first = pair * groups_pair
-        sent_ref[pl.ds(first, groups_pair)] = chunks.astype(bf16).reshape(
+        sent_ref[first : first + groups_pair] = chunks.astype(bf16).reshape(
             groups_pair, owners, CHUNK, LANES
         )
 
@@ -366,8 +451,25 @@
                 there_copy(first + step, place).start()
             stick_ref[first + step, me] = sent_ref[first + step, me]
 
-    main_copy.wait()
-    rest_copy.wait()
+    for pair in range(pairs):
+        scatter_waves(pair)
+
+    freq_x = jnp.where(grid_x >= half, grid_x - size, grid_x)
+    freq_y = jnp.where(grid_y >= half, grid_y - size, grid_y)
+    freq_row = lax.broadcasted_iota(jnp.int32, (16, LANES), 0)
+    freqs = jnp.where(freq_row == 0, freq_x, jnp.where(freq_row == 1, freq_y, 0.0))
+    freqs = jnp.concatenate([freqs, freqs], axis=1).astype(bf16)
+
+    @pl.loop(0, blocks // 8)
+    def _(step):
+        found = dot(freqs, hot_ref[:, lanes_of(8 * step, 8)])
+        plane = lax.shift_right_logical(slot_ref[:, lanes_of(8 * step, 8)], 7)
+        freq_z = jnp.where(plane >= half, plane - size, plane).astype(f32)
+        total = freq_z * freq_z + found[0:1] * found[0:1] + found[1:2] * found[1:2]
+        kinetic_ref[:, lanes_of(8 * step, 8)] = total * (2.0 / (size * size))
+
+    for place in range(1, len(loads)):
+        loads[place].wait()
 
     @pl.loop(0, slab)
     def _(plane):
@@ -391,6 +493,44 @@
             there_ref[owner, part * sticks : (part + 1) * sticks, :] = rows.astype(bf16)
             turned = dot(turn_ref[part], hot)
             again_ref[owner, :, part * sticks : (part + 1) * sticks] = turned.astype(bf16)
+
+    for place in range(mesh_bands - 1):
+        band_copy(place).wait()
+
+    count = mesh_bands * bands
+    others_side = every_ref[...].reshape(count, 2, waves).astype(f32)
+    right_side_ref[:count] = others_side[:, 0].astype(bf16)
+    right_side_ref[count : 2 * count] = others_side[:, 1].astype(bf16)
+    own_side = subspace_ref[...].astype(f32)
+    own_side = jnp.concatenate([own_side[:, 0], own_side[:, 1]], axis=0).astype(bf16)
+    products = lax.dot_general(
+        own_side, right_side_ref[...], (((1,), (1,)), ((), ())), preferred_element_type=f32
+    )
+    lane = lax.broadcasted_iota(jnp.int32, (1, LANES), 1)
+    upper, lower = products[:mine], products[mine:]
+    blend = jnp.where(
+        lane < count,
+        upper + pltpu.roll(lower, LANES - count, 1),
+        upper - pltpu.roll(lower, count, 1),
+    )
+    for block in range(shares):
+        share_ref[block] = blend[block * share : (block + 1) * share]
+
+    source_band = lax.div(me, shares)
+    for block in range(shares):
+        for place in range(mesh_bands):
+            if place:
+                share_copy(block, place).start()
+            else:
+                to_self = shares * band_me + block == me
+
+                @pl.when(jnp.logical_not(to_self))
+                def _():
+                    share_copy(block, place).start()
+
+                @pl.when(to_self)
+                def _():
+                    shares_ref[me] = share_ref[block]
 
     def spread_lines(group):
         for low in range(half_owners):
@@ -558,11 +698,7 @@
     picked_lines(groups + 1)
     send_home(groups - 1)
 
-    for place in range(owners - 1):
-        extra_copy(place).wait()
-
-    @pl.loop(0, pairs)
-    def _(pair):
+    def gather_waves(pair):
         first = pair * groups_pair
 
         @pl.loop(0, groups_pair)
@@ -570,7 +706,7 @@
             for place in range(owners - 1):
                 home_copy(first + step, place).wait()
 
-        chunks = back_ref[pl.ds(first, groups_pair)].reshape(groups_pair * owners, CHUNK, LANES)
+        chunks = back_ref[first : first + groups_pair].reshape(groups_pair * owners, CHUNK, LANES)
         chunks = chunks.astype(f32)
         columns = []
         for band in range(PAIR):
@@ -586,31 +722,61 @@
                     start = part * size + side * half
                     both.append(risen[start : start + half, band * LANES : (band + 1) * LANES])
                 pieces.append(jnp.concatenate(both, axis=1))
-        spread_ref[:, : 2 * LANES] = jnp.concatenate(pieces, axis=0)
-
-        @pl.loop(0, blocks // 2, unroll=2)
+        gather_ref[...] = jnp.concatenate(pieces, axis=0)
+
+        @pl.loop(0, blocks // 2, unroll=4)
         def _(step):
-            place = pl.ds(pl.multiple_of(step * 2 * LANES, LANES), 2 * LANES)
-            values = dot(spread_ref[:, : 2 * LANES], hot_ref[:, place])
+            values = dot(gather_ref[...], hot_ref[:, lanes_of(2 * step, 2)])
             for side in range(2):
-                block = 2 * step + side
-                chosen = level_mask(block)
+                chosen = level_mask(2 * step + side)
                 for part in range(2 * PAIR):
-                    mine = values[part * half : (part + 1) * half, side * LANES : (side + 1) * LANES]
-                    out_ref[2 * PAIR * pair + part, pl.ds(block, 1), :] = jnp.sum(
-                        jnp.where(chosen, mine, 0.0), axis=0, keepdims=True
+                    ours = values[part * half : (part + 1) * half, side * LANES : (side + 1) * LANES]
+                    row = 2 * PAIR * pair + part
+                    found_ref[row : row + 1, lanes_of(2 * step + side)] = jnp.sum(
+                        jnp.where(chosen, ours, 0.0), axis=0, keepdims=True
                     )
 
-
-def whole_work(waves, slots, coords, extra, potential):
+    for pair in range(pairs):
+        gather_waves(pair)
+
+    result = found_ref[...] + kinetic_ref[...] * wave_ref[...]
+    applied_ref[...] = result.astype(bf16).reshape(bands, 2, waves)
+
+    for block in range(shares):
+        for place in range(mesh_bands):
+            if place:
+                share_copy(block, place).wait_send()
+            else:
+
+                @pl.when(shares * band_me + block != me)
+                def _():
+                    share_copy(block, place).wait_send()
+
+    for source in range(owners):
+        from_self = jnp.logical_and(source_band == band_me, me == source)
+
+        @pl.when(jnp.logical_not(from_self))
+        def _():
+            share_arrival(source).wait_recv()
+
+    total = shares_ref[0]
+    for source in range(1, owners):
+        total = total + shares_ref[source]
+    total = pltpu.roll(total, lax.rem(LANES - bands * band_me, LANES), 1)
+    inter_ref[0] = total[:, :bands]
+    inter_ref[1] = total[:, count : count + bands]
+
+
+def whole_work(mesh_bands, orbitals, slots, columns, potential, subspace, previous):
     slab, size, _ = potential.shape
     owners = size // slab
     groups_pair = slab // PLANES
-    parts, blocks, _ = waves.shape
-    pairs = parts // (2 * PAIR)
-    groups = pairs * groups_pair
+    bands, _, waves = orbitals.shape
+    groups = bands // PAIR * groups_pair
     half = size // 2
     lines = PLANES * PAIR
+    mine = subspace.shape[0]
+    share = mine * mesh_bands // owners
     deep, rise = column_tables(size, slab)
     line, turn = line_tables(size)
     halves = half_tables(size)
@@ -620,21 +786,31 @@
     bf16, f32 = jnp.bfloat16, jnp.float32
     dma = pltpu.SemaphoreType.DMA
     return pl.pallas_call(
-        whole_kernel,
+        functools.partial(whole_kernel, mesh_bands),
         out_shape=(
-            jax.ShapeDtypeStruct(waves.shape, f32),
-            jax.ShapeDtypeStruct(extra.shape, bf16),
+            jax.ShapeDtypeStruct(orbitals.shape, bf16),
+            jax.ShapeDtypeStruct((2, share, bands), f32),
         ),
-        in_specs=[in_vmem] * 4 + [anywhere] + [in_vmem] * 6,
+        in_specs=[in_vmem] * 4 + [anywhere] * 7 + [in_vmem],
         out_specs=(in_vmem, in_vmem),
         scratch_shapes=[
+            pltpu.VMEM(subspace.shape, bf16),
+            pltpu.VMEM(deep.shape, bf16),
+            pltpu.VMEM(rise.shape, bf16),
+            pltpu.VMEM(line.shape, bf16),
+            pltpu.VMEM(turn.shape, bf16),
+            pltpu.VMEM(halves.shape, bf16),
             pltpu.VMEM((slab, size, size), f32),
             pltpu.VMEM((slab, size, LANES), f32),
             pltpu.VMEM((slab, size, LANES), f32),
-            pltpu.VMEM((2 * LANES, blocks * LANES), bf16),
-            pltpu.VMEM((2 * PAIR * half, blocks * LANES), bf16),
+            pltpu.VMEM((2 * bands, waves), f32),
+            pltpu.VMEM((2 * bands, waves), f32),
+            pltpu.VMEM((1, waves), f32),
+            pltpu.VMEM((2 * LANES, waves), bf16),
+            pltpu.VMEM((2 * PAIR * half, 2 * LANES), bf16),
             pltpu.VMEM((groups, owners, CHUNK, LANES), bf16),
             pltpu.VMEM((groups, owners, CHUNK, LANES), bf16),
+            pltpu.VMEM((8, LANES), f32),
             pltpu.VMEM((owners, 8, LANES), f32),
             pltpu.VMEM((owners, slab, LANES), f32),
             pltpu.VMEM((owners, 2 * LANES, 4 * LANES), bf16),
@@ -645,110 +821,63 @@
             pltpu.VMEM((owners, lines * slab, 2 * LANES), bf16),
             pltpu.VMEM((groups + 2, owners, CHUNK, LANES), bf16),
             pltpu.VMEM((groups, owners, CHUNK, LANES), bf16),
-            dma((2,)),
+            pltpu.VMEM((mesh_bands, bands, 2, waves), bf16),
+            pltpu.VMEM((LANES, waves), bf16),
+            pltpu.VMEM((mine // share, share, LANES), f32),
+            pltpu.VMEM((owners, share, LANES), f32),
+            dma((8,)),
             dma((groups, owners - 1)),
             dma((groups, owners - 1)),
             dma((groups, owners - 1)),
             dma((groups, owners - 1)),
-            dma((2, owners - 1)),
-            dma((2, owners - 1)),
+            dma((owners - 1,)),
+            dma((owners - 1,)),
+            dma((mesh_bands - 1,)),
+            dma((mesh_bands - 1,)),
+            dma((mine // share, mesh_bands)),
+            dma((owners,)),
         ],
         compiler_params=pltpu.CompilerParams(
-            collective_id=0, has_side_effects=True, vmem_limit_bytes=56 * 1024 * 1024
+            collective_id=0, has_side_effects=True, vmem_limit_bytes=60 * 1024 * 1024
         ),
         cost_estimate=pl.CostEstimate(
             flops=40 * 10**9, bytes_accessed=8 * 10**6, transcendentals=0
         ),
-    )(waves, slots, coords, extra, potential, deep, rise, line, turn, halves, pick)
-
-
-def gathered_bands(array, mesh_bands):
-    here = lax.axis_index("band")
-    blocks = [array]
-    for shift in range(1, mesh_bands):
-        pairs = [((src + shift) % mesh_bands, src) for src in range(mesh_bands)]
-        blocks.append(lax.ppermute(array, "band", pairs))
-    return blocks, here
-
-
-def overlaps(subspace, previous, mesh_bands, owners):
-    blocks, here = gathered_bands(subspace, mesh_bands)
-    prev_real, prev_imag = previous[:, 0], previous[:, 1]
-    right = jnp.concatenate(
-        [
-            jnp.concatenate([prev_real, prev_imag], axis=1),
-            jnp.concatenate([prev_imag, -prev_real], axis=1),
-        ],
-        axis=0,
+    )(
+        orbitals,
+        slots,
+        columns,
+        previous,
+        subspace,
+        potential,
+        deep,
+        rise,
+        line,
+        turn,
+        halves,
+        pick,
     )
-    partials = []
-    for block in blocks:
-        partials.append(
-            jnp.einsum(
-                "jg,ig->ji",
-                block.reshape(block.shape[0], -1),
-                right,
-                preferred_element_type=jnp.float32,
-            )
-        )
-    twice = jnp.concatenate(partials + partials, axis=0)
-    count = twice.shape[0] // 2
-    start = (count - here * subspace.shape[0]) % count
-    ordered = lax.dynamic_slice_in_dim(twice, start, count, axis=0)
-    split = ordered.reshape(owners, count // owners, 2, previous.shape[0])
-    return split.transpose(0, 2, 1, 3)
 
 
 def fast_device(mesh_bands, orbitals, sphere_slot, stick_column, potential, subspace, previous):
-    slab_depth, grid_size, _ = potential.shape
-    stick_count = stick_column.shape[0]
-    owners = grid_size // slab_depth
-    bands = orbitals.shape[0]
-    plane_index = sphere_slot // stick_count
-    stick_index = sphere_slot % stick_count
-    stick_hot = one_hot_rows(stick_index, stick_count)
-    stick_x = stick_column // grid_size
-    stick_y = stick_column % grid_size
-    stick_coords = jnp.stack([stick_x, stick_y]).astype(jnp.bfloat16)
-    wave_coords = jnp.dot(stick_coords, stick_hot, preferred_element_type=jnp.float32)
-    freq_z = frequency(plane_index, grid_size)
-    freq_x = frequency(wave_coords[0].astype(jnp.int32), grid_size)
-    freq_y = frequency(wave_coords[1].astype(jnp.int32), grid_size)
-    kinetic = (freq_z * freq_z + freq_x * freq_x + freq_y * freq_y) * (
-        2.0 / (grid_size * grid_size)
-    )
-    local_x = stick_x - lax.axis_index("fft") * slab_depth
-    coords = jnp.stack([local_x, stick_y]).astype(jnp.float32)
-    coords = jnp.pad(coords, ((0, 8 - 2), (0, 0)))
-    split = overlaps(subspace, previous, mesh_bands, owners)
-    flat = split.reshape(owners, 1, -1)
-    high = lax.reduce_precision(flat, 8, 7)
-    low = lax.reduce_precision(flat - high, 8, 7)
-    both = jnp.concatenate([high, low], axis=2).astype(jnp.bfloat16)
-    width = both.shape[2]
-    lanes = -(-width // stick_count) * stick_count
-    both = jnp.pad(both, ((0, 0), (0, 0), (0, lanes - width)))
-    both = both.reshape(owners, -1, stick_count)
-    both = jnp.pad(both, ((0, 0), (0, EXTRA - both.shape[1]), (0, 0)))
-    waves = orbitals.astype(jnp.float32).reshape(2 * bands, -1, LANES)
-    slots = sphere_slot.reshape(-1, LANES)
-    found, returned = whole_work(waves, slots, coords, both, potential)
-    sums = returned.reshape(owners, -1)[:, :width].astype(jnp.float32)
-    sums = jnp.sum(sums, axis=0)
-    intersection = (sums[: width // 2] + sums[width // 2 :]).reshape(split.shape[1:])
-    found = found.reshape(orbitals.shape)
-    applied = (found + kinetic * orbitals.astype(jnp.float32)).astype(jnp.bfloat16)
-    return (applied, intersection)
-
-
-def per_device(mesh_bands, *arrays):
-    orbitals, slots, sticks, potential, _, _ = arrays
+    slots = sphere_slot.reshape(1, -1)
+    columns = stick_column.reshape(1, -1)
+    return whole_work(mesh_bands, orbitals, slots, columns, potential, subspace, previous)
+
+
+def fits(mesh_bands, orbitals, slots, sticks, potential, subspace, previous):
     slab, size, _ = potential.shape
     owners = size // slab
-    fits = slab % 8 == 0 and owners % 2 == 0 and owners * slab == size
-    fits = fits and 2 * size == 3 * LANES and sticks.shape[0] == LANES
-    fits = fits and orbitals.shape[0] % PAIR == 0 and slots.shape[0] % (2 * LANES) == 0
-    if fits:
+    bands, mine = orbitals.shape[0], subspace.shape[0]
+    good = slab % 8 == 0 and owners % 2 == 0 and owners * slab == size
+    good = good and 2 * size == 3 * LANES and sticks.shape[0] == LANES
+    good = good and bands % PAIR == 0 and slots.shape[0] % (8 * LANES) == 0
+    good = good and mine * mesh_bands % (8 * owners) == 0 and owners % mesh_bands == 0
+    return good and 2 * mesh_bands * bands <= LANES
+
+
+def per_device(mesh_bands, *arrays):
+    if fits(mesh_bands, *arrays):
         return fast_device(mesh_bands, *arrays)
     return general_device(*arrays)
 

time: 72.4 us -> 57.9 us (0.80)
  starting transfers between devices: 4.48 us -> 0 us
  local copies, waits for them, and re-layouts: 6.85 us -> 2.88 us
  other arithmetic: 3.75 us -> 0 us
  waiting for transfers between devices: 3.44 us -> 0 us
  Pallas kernels: 51.4 us -> 54.1 us
  matrix products: 1.25 us -> 0 us
    ppermute x3 -> x0, starting transfers between devices: 4.48 us -> none  [gathered_bands(): blocks.append(lax.ppermute(array, 'band', pairs))]
    ppermute x3 -> x0, waiting for transfers between devices: 3.44 us -> none  [gathered_bands(): blocks.append(lax.ppermute(array, 'band', pairs))]
    pallas_call x1, Pallas kernels: 51.4 us -> 54.1 us  [whole_work(): pl.pallas_call(functools.partial(whole_kernel, mesh_bands), out_shape=(ja...]
    reshape x4 -> x0, local copies, waits for them, and re-layouts: 1.8 us -> none  [the longest x1 0.97 us: fast_device(): found = found.reshape(orbitals.shape)]
    unnamed x9 -> x1, local copies, waits for them, and re-layouts: 3.07 us -> 1.51 us
    pallas_call x0 -> x1, local copies, waits for them, and re-layouts: none -> 1.37 us  [whole_work(): pl.pallas_call(functools.partial(whole_kernel, mesh_bands), out_shape=(ja...]
    dot_general x5 -> x0, matrix products: 1.25 us -> none  [the longest x4 0.82 us: overlaps(): jnp.einsum('jg,ig->ji', block.reshape(block.shape[0], -1), right, preferr...]
    slice x1 -> x0, local copies, waits for them, and re-layouts: 1.03 us -> none  [overlaps(): prev_real, prev_imag = (previous[:, 0], previous[:, 1])]
  transfers between devices with their start and end apart: 3 -> 0, of which waited for: 1 -> 0; matrix products, arithmetic and copies ran while one was open for 10% -> 0% of each run, Pallas kernels for 0% -> 0%
where the time goes in v2:
time: 57.9 us; the launch traced here: 57.7 us
  Pallas kernels  54.1 us (93%)
  local copies, waits for them, and re-layouts  2.88 us (5%)
  between operations  0.64 us (1%)
    pallas_call x1, Pallas kernels, whole_work(): pl.pallas_call(functools.partial(whole_kernel, mesh_bands), out_shape=(ja...  54.1 us
    unnamed x1, local copies, waits for them, and re-layouts  1.51 us
    pallas_call x1, local copies, waits for them, and re-layouts, whole_work(): pl.pallas_call(functools.partial(whole_kernel, mesh_bands), out_shape=(ja...  1.37 us

profile of v2, /device:TPU:0, one launch (start us, length us, event | category | flops | bytes accessed | tf_op | source)
XLA Modules:
  0.0 57.7 jit_solution(17656875104284197311)
XLA Ops:
  0.6 54.1 %shard_map.131 = (bf16[4,2,4096]{2,1,0:T(2,128)(2,1)}, f32[2,8,4]{2,1,0:T(8,128)}) custom-call(bf16[4,2,4096]{2,1,0:T(2,128)(2,1)} %orbital_ref.1, s32[1,4096]{1,0:T(1,128)} %bitcast.2, s32[1,128]{1,0:T(1,128)} %bitcast.3, bf16[4,2,4096]{2,1,0:T(2,128)(2,1)} %previous_ref.1, bf16[16,2,4096]{2,1,0:T(2,128)(2,1)} %subspace_hbm.1, f32[24,192,192]{2,1,0:T(8,128)} %pot_ref.1, ...), custom_call_target="tpu_custom_call" | custom-call | flops 40000000000 | bytes 8000000 | tf_op jit(solution)/shard_map/pallas_call | solution.py:788
  54.8 1.4 %copy.14 = f32[2,8,4]{1,2,0:T(4,128)} copy(f32[2,8,4]{2,1,0:T(8,128)} %get-tuple-element.3) | data formatting | bytes 512 | tf_op jit(solution)/shard_map/pallas_call | solution.py:788
  56.1 1.5 %copy.16 = bf16[4,2,4096]{2,1,0:T(2,128)(2,1)} copy(bf16[4,2,4096]{2,1,0:T(2,128)(2,1)} %get-tuple-element.6) | data formatting | bytes 131072

commit v3 on v2

--- a/solution.py
+++ b/solution.py
@@ -132,7 +132,7 @@
 PAIR = 2
 LANES = 128
 CHUNK = 4 * PLANES
-EXTRA = 16
+FOLD = 4
 
 
 def phases(products, length):
@@ -242,21 +242,15 @@
     share_ref,
     shares_ref,
     load_sem,
-    send_sem,
     recv_sem,
-    home_send,
     home_recv,
-    coord_send,
-    coord_recv,
-    band_send,
-    band_recv,
-    share_send,
-    share_recv,
+    once_sem,
 ):
     slab, size, _ = pot_ref.shape
     owners = size // slab
     half_owners = owners // 2
     half = size // 2
+    fold = size // FOLD
     groups_pair = slab // PLANES
     waves = slot_ref.shape[1]
     blocks = waves // LANES
@@ -279,6 +273,9 @@
     def dot(left, right):
         return jnp.dot(left, right, preferred_element_type=f32)
 
+    def halves_dot(table_ref, right):
+        return jnp.concatenate([dot(table_ref[:size], right), dot(table_ref[size:], right)], axis=0)
+
     def remote(src, dst, send, recv, target):
         return pltpu.make_async_remote_copy(
             src_ref=src,
@@ -293,8 +290,8 @@
         return remote(
             coord_ref,
             coords_ref.at[me],
-            coord_send.at[place],
-            coord_recv.at[place],
+            once_sem.at[0],
+            once_sem.at[1],
             {"fft": others[place]},
         )
 
@@ -302,8 +299,8 @@
         return remote(
             previous_ref,
             every_ref.at[band_me],
-            band_send.at[place],
-            band_recv.at[place],
+            once_sem.at[2],
+            once_sem.at[3],
             {"band": every_band[place + 1]},
         )
 
@@ -311,26 +308,20 @@
         return remote(
             share_ref.at[block],
             shares_ref.at[me],
-            share_send.at[block, place],
-            share_recv.at[me],
+            once_sem.at[4],
+            once_sem.at[5],
             {"band": every_band[place], "fft": shares * band_me + block},
         )
 
-    def share_arrival(source):
-        return remote(
-            share_ref.at[0],
-            shares_ref.at[source],
-            share_send.at[0, 0],
-            share_recv.at[source],
-            {"fft": others[0]},
-        )
+    def await_bytes(region, sem):
+        pltpu.make_async_copy(region, region, sem).wait()
 
     def there_copy(group, place):
         return remote(
             sent_ref.at[group, others[place]],
             stick_ref.at[group, me],
-            send_sem.at[group, place],
-            recv_sem.at[group, place],
+            once_sem.at[6],
+            recv_sem.at[group],
             {"fft": others[place]},
         )
 
@@ -338,8 +329,8 @@
         return remote(
             stage_ref.at[group + 2, others[place]],
             back_ref.at[group, me],
-            home_send.at[group, place],
-            home_recv.at[group, place],
+            once_sem.at[7],
+            home_recv.at[group],
             {"fft": others[place]},
         )
 
@@ -371,7 +362,7 @@
                 )
 
     low_lane = lax.broadcasted_iota(jnp.int32, (1, LANES), 1) < rest
-    level = lax.broadcasted_iota(jnp.int32, (half, LANES), 0)
+    level = lax.broadcasted_iota(jnp.int32, (fold, LANES), 0)
     wave_ref[...] = orbital_ref[...].reshape(2 * bands, waves).astype(f32)
 
     column = column_ref[...]
@@ -390,8 +381,11 @@
     @pl.loop(0, blocks, unroll=4)
     def _(block):
         slot = slot_ref[:, lanes_of(block)]
-        cell = jnp.where(plane_of(block) >= half, sticks, 0) + jnp.bitwise_and(slot, sticks - 1)
-        rows = lax.broadcasted_iota(jnp.int32, (2 * sticks, LANES), 0)
+        plane = plane_of(block)
+        cell = jnp.bitwise_and(slot, sticks - 1)
+        for side in range(1, FOLD):
+            cell = cell + jnp.where(plane >= side * fold, sticks, 0)
+        rows = lax.broadcasted_iota(jnp.int32, (FOLD * sticks, LANES), 0)
         hot_ref[:, lanes_of(block)] = jnp.where(cell == rows, 1.0, 0.0).astype(bf16)
 
     pl.semaphore_wait(barrier, mesh_bands * owners - 1)
@@ -404,61 +398,58 @@
 
     def level_mask(block):
         plane = plane_of(block)
-        return jnp.where(plane >= half, plane - half, plane) == level
-
-    def scatter_waves(pair):
-        cells = None
-        for block in range(0, blocks, 2):
-            pieces = []
-            for step in range(2):
-                chosen = level_mask(block + step)
-                values = wave_ref[
-                    2 * PAIR * pair : 2 * PAIR * (pair + 1), lanes_of(block + step)
-                ]
-                rows = []
-                for part in range(2 * PAIR):
-                    rows.append(jnp.where(chosen, values[part : part + 1], 0.0))
-                pieces.append(jnp.concatenate(rows, axis=0))
-            left = jnp.concatenate(pieces, axis=1).astype(bf16)
-            term = lax.dot_general(
-                left,
-                hot_ref[:, lanes_of(block, 2)],
-                (((1,), (1,)), ((), ())),
-                preferred_element_type=f32,
-            )
-            cells = term if cells is None else cells + term
-        columns = []
-        for band in range(PAIR):
-            pieces = []
-            for part in range(2):
-                start = (2 * band + part) * half
-                for side in range(2):
-                    pieces.append(cells[start : start + half, side * LANES : (side + 1) * LANES])
-            columns.append(jnp.concatenate(pieces, axis=0))
-        columns = jnp.concatenate(columns, axis=1).astype(bf16)
-        if pair == 0:
-            loads[0].wait()
-        along = dot(deep_ref[...], columns).reshape(groups_pair * owners, 2 * PLANES, PAIR * LANES)
-        chunks = jnp.concatenate([along[:, :, :LANES], along[:, :, LANES:]], axis=1)
-        first = pair * groups_pair
-        sent_ref[first : first + groups_pair] = chunks.astype(bf16).reshape(
-            groups_pair, owners, CHUNK, LANES
+        for side in range(1, FOLD):
+            base = jnp.where(plane >= side * fold, side * fold, 0 if side == 1 else base)
+        return plane - base == level
+
+    cells = None
+    for block in range(0, blocks, 2):
+        pieces = []
+        for step in range(2):
+            chosen = level_mask(block + step)
+            values = wave_ref[:, lanes_of(block + step)]
+            rows = [jnp.where(chosen, values[row : row + 1], 0.0) for row in range(2 * bands)]
+            pieces.append(jnp.concatenate(rows, axis=0))
+        left = jnp.concatenate(pieces, axis=1).astype(bf16)
+        term = lax.dot_general(
+            left,
+            hot_ref[:, lanes_of(block, 2)],
+            (((1,), (1,)), ((), ())),
+            preferred_element_type=f32,
         )
-
-        @pl.loop(0, groups_pair)
-        def _(step):
-            for place in range(owners - 1):
-                there_copy(first + step, place).start()
-            stick_ref[first + step, me] = sent_ref[first + step, me]
-
+        cells = term if cells is None else cells + term
+    columns = []
+    for band in range(bands):
+        pieces = []
+        for part in range(2):
+            start = (2 * band + part) * fold
+            for side in range(FOLD):
+                pieces.append(cells[start : start + fold, side * LANES : (side + 1) * LANES])
+        columns.append(jnp.concatenate(pieces, axis=0))
+    columns = jnp.concatenate(columns, axis=1).astype(bf16)
+    loads[0].wait()
+    along = dot(deep_ref[...], columns).reshape(groups_pair * owners, 2 * PLANES, bands * LANES)
     for pair in range(pairs):
-        scatter_waves(pair)
+        chunks = []
+        for band in range(PAIR * pair, PAIR * (pair + 1)):
+            chunks.append(along[:, :, band * LANES : (band + 1) * LANES])
+        sent_ref[pair * groups_pair : (pair + 1) * groups_pair] = (
+            jnp.concatenate(chunks, axis=1)
+            .astype(bf16)
+            .reshape(groups_pair, owners, CHUNK, LANES)
+        )
+
+    @pl.loop(0, groups)
+    def _(group):
+        for place in range(owners - 1):
+            there_copy(group, place).start()
+        stick_ref[group, me] = sent_ref[group, me]
 
     freq_x = jnp.where(grid_x >= half, grid_x - size, grid_x)
     freq_y = jnp.where(grid_y >= half, grid_y - size, grid_y)
     freq_row = lax.broadcasted_iota(jnp.int32, (16, LANES), 0)
     freqs = jnp.where(freq_row == 0, freq_x, jnp.where(freq_row == 1, freq_y, 0.0))
-    freqs = jnp.concatenate([freqs, freqs], axis=1).astype(bf16)
+    freqs = jnp.concatenate([freqs] * FOLD, axis=1).astype(bf16)
 
     @pl.loop(0, blocks // 8)
     def _(step):
@@ -471,31 +462,35 @@
     for place in range(1, len(loads)):
         loads[place].wait()
 
-    @pl.loop(0, slab)
+    @pl.loop(0, slab, unroll=4)
     def _(plane):
         local = full_ref[plane, :, LANES:]
         right_ref[plane] = jnp.concatenate([local, local], axis=1)
 
-    for place in range(owners - 1):
-        coord_copy(place).wait()
-
-    @pl.loop(0, owners)
-    def _(owner):
-        coords = coords_ref[owner]
+    await_bytes(coords_ref.at[: owners - 1], once_sem.at[1])
+
+    @pl.loop(0, owners // 2, unroll=2)
+    def _(step):
         local = lax.broadcasted_iota(jnp.int32, (slab, sticks), 0).astype(f32)
-        mask_ref[owner] = jnp.where(coords[0:1, :] == local, 1.0, 0.0)
         cells = lax.broadcasted_iota(jnp.int32, (size, sticks), 0).astype(f32)
-        hot = jnp.where(coords[1:2, :] == cells, 1.0, 0.0).astype(bf16)
+        hots = []
+        for side in range(2):
+            coords = coords_ref[2 * step + side]
+            mask_ref[2 * step + side] = jnp.where(coords[0:1, :] == local, 1.0, 0.0)
+            hots.append(jnp.where(coords[1:2, :] == cells, 1.0, 0.0))
+        hot = jnp.concatenate(hots, axis=1).astype(bf16)
         for part in range(2):
+            place = slice(part * sticks, (part + 1) * sticks)
             rows = lax.dot_general(
                 hot, line_ref[part], (((0,), (0,)), ((), ())), preferred_element_type=f32
-            )
-            there_ref[owner, part * sticks : (part + 1) * sticks, :] = rows.astype(bf16)
-            turned = dot(turn_ref[part], hot)
-            again_ref[owner, :, part * sticks : (part + 1) * sticks] = turned.astype(bf16)
-
-    for place in range(mesh_bands - 1):
-        band_copy(place).wait()
+            ).astype(bf16)
+            turned = dot(turn_ref[part], hot).astype(bf16)
+            for side in range(2):
+                mine_here = slice(side * sticks, (side + 1) * sticks)
+                there_ref[2 * step + side, place, :] = rows[mine_here]
+                again_ref[2 * step + side, :, place] = turned[:, mine_here]
+
+    await_bytes(every_ref.at[: mesh_bands - 1], once_sem.at[3])
 
     count = mesh_bands * bands
     others_side = every_ref[...].reshape(count, 2, waves).astype(f32)
@@ -663,8 +658,7 @@
             ).astype(bf16)
 
     def wait_group(group):
-        for place in range(owners - 1):
-            there_copy(group, place).wait()
+        await_bytes(stick_ref.at[group, : owners - 1], recv_sem.at[group])
 
     def send_home(group):
         for place in range(owners - 1):
@@ -703,8 +697,7 @@
 
         @pl.loop(0, groups_pair)
         def _(step):
-            for place in range(owners - 1):
-                home_copy(first + step, place).wait()
+            await_bytes(back_ref.at[first + step, : owners - 1], home_recv.at[first + step])
 
         chunks = back_ref[first : first + groups_pair].reshape(groups_pair * owners, CHUNK, LANES)
         chunks = chunks.astype(f32)
@@ -713,15 +706,15 @@
             rows = chunks[:, band * 2 * PLANES : (band + 1) * 2 * PLANES]
             columns.append(rows.reshape(2 * size, LANES))
         columns = jnp.concatenate(columns, axis=1).astype(bf16)
-        risen = (dot(rise_ref[...], columns) * (1.0 / size)).astype(bf16)
+        risen = (halves_dot(rise_ref, columns) * (1.0 / size)).astype(bf16)
         pieces = []
         for band in range(PAIR):
             for part in range(2):
-                both = []
-                for side in range(2):
-                    start = part * size + side * half
-                    both.append(risen[start : start + half, band * LANES : (band + 1) * LANES])
-                pieces.append(jnp.concatenate(both, axis=1))
+                sides = []
+                for side in range(FOLD):
+                    start = part * size + side * fold
+                    sides.append(risen[start : start + fold, band * LANES : (band + 1) * LANES])
+                pieces.append(jnp.concatenate(sides, axis=1))
         gather_ref[...] = jnp.concatenate(pieces, axis=0)
 
         @pl.loop(0, blocks // 2, unroll=4)
@@ -730,7 +723,7 @@
             for side in range(2):
                 chosen = level_mask(2 * step + side)
                 for part in range(2 * PAIR):
-                    ours = values[part * half : (part + 1) * half, side * LANES : (side + 1) * LANES]
+                    ours = values[part * fold : (part + 1) * fold, side * LANES : (side + 1) * LANES]
                     row = 2 * PAIR * pair + part
                     found_ref[row : row + 1, lanes_of(2 * step + side)] = jnp.sum(
                         jnp.where(chosen, ours, 0.0), axis=0, keepdims=True
@@ -742,29 +735,28 @@
     result = found_ref[...] + kinetic_ref[...] * wave_ref[...]
     applied_ref[...] = result.astype(bf16).reshape(bands, 2, waves)
 
-    for block in range(shares):
-        for place in range(mesh_bands):
-            if place:
-                share_copy(block, place).wait_send()
-            else:
-
-                @pl.when(shares * band_me + block != me)
-                def _():
-                    share_copy(block, place).wait_send()
-
-    for source in range(owners):
-        from_self = jnp.logical_and(source_band == band_me, me == source)
-
-        @pl.when(jnp.logical_not(from_self))
-        def _():
-            share_arrival(source).wait_recv()
+    inside = source_band == band_me
+
+    @pl.when(inside)
+    def _():
+        await_bytes(shares_ref.at[: mesh_bands * shares - 1], once_sem.at[4])
+        await_bytes(shares_ref.at[: owners - 1], once_sem.at[5])
+
+    @pl.when(jnp.logical_not(inside))
+    def _():
+        await_bytes(shares_ref.at[: mesh_bands * shares], once_sem.at[4])
+        await_bytes(shares_ref, once_sem.at[5])
+
+    await_bytes(coords_ref.at[: owners - 1], once_sem.at[0])
+    await_bytes(every_ref.at[: mesh_bands - 1], once_sem.at[2])
+    await_bytes(stick_ref.at[:, : owners - 1], once_sem.at[6])
+    await_bytes(back_ref.at[:, : owners - 1], once_sem.at[7])
 
     total = shares_ref[0]
     for source in range(1, owners):
         total = total + shares_ref[source]
     total = pltpu.roll(total, lax.rem(LANES - bands * band_me, LANES), 1)
-    inter_ref[0] = total[:, :bands]
-    inter_ref[1] = total[:, count : count + bands]
+    inter_ref[...] = total
 
 
 def whole_work(mesh_bands, orbitals, slots, columns, potential, subspace, previous):
@@ -789,7 +781,7 @@
         functools.partial(whole_kernel, mesh_bands),
         out_shape=(
             jax.ShapeDtypeStruct(orbitals.shape, bf16),
-            jax.ShapeDtypeStruct((2, share, bands), f32),
+            jax.ShapeDtypeStruct((share, LANES), f32),
         ),
         in_specs=[in_vmem] * 4 + [anywhere] * 7 + [in_vmem],
         out_specs=(in_vmem, in_vmem),
@@ -806,8 +798,8 @@
             pltpu.VMEM((2 * bands, waves), f32),
             pltpu.VMEM((2 * bands, waves), f32),
             pltpu.VMEM((1, waves), f32),
-            pltpu.VMEM((2 * LANES, waves), bf16),
-            pltpu.VMEM((2 * PAIR * half, 2 * LANES), bf16),
+            pltpu.VMEM((FOLD * LANES, waves), bf16),
+            pltpu.VMEM((2 * PAIR * size // FOLD, FOLD * LANES), bf16),
             pltpu.VMEM((groups, owners, CHUNK, LANES), bf16),
             pltpu.VMEM((groups, owners, CHUNK, LANES), bf16),
             pltpu.VMEM((8, LANES), f32),
@@ -826,16 +818,9 @@
             pltpu.VMEM((mine // share, share, LANES), f32),
             pltpu.VMEM((owners, share, LANES), f32),
             dma((8,)),
-            dma((groups, owners - 1)),
-            dma((groups, owners - 1)),
-            dma((groups, owners - 1)),
-            dma((groups, owners - 1)),
-            dma((owners - 1,)),
-            dma((owners - 1,)),
-            dma((mesh_bands - 1,)),
-            dma((mesh_bands - 1,)),
-            dma((mine // share, mesh_bands)),
-            dma((owners,)),
+            dma((groups,)),
+            dma((groups,)),
+            dma((8,)),
         ],
         compiler_params=pltpu.CompilerParams(
             collective_id=0, has_side_effects=True, vmem_limit_bytes=60 * 1024 * 1024
@@ -859,10 +844,34 @@
     )
 
 
+def hand_out(bands, count, applied_in, total_in, applied_ref, inter_ref):
+    applied_ref[...] = applied_in[...]
+    total = total_in[...].T
+    inter_ref[0] = total[:bands]
+    inter_ref[1] = total[count : count + bands]
+
+
+def handed_out(mesh_bands, applied, total):
+    bands, share = applied.shape[0], total.shape[0]
+    in_vmem = pl.BlockSpec(memory_space=pltpu.VMEM)
+    return pl.pallas_call(
+        functools.partial(hand_out, bands, mesh_bands * bands),
+        out_shape=(
+            jax.ShapeDtypeStruct(applied.shape, jnp.bfloat16),
+            jax.ShapeDtypeStruct((2, bands, share), jnp.float32),
+        ),
+        in_specs=[in_vmem] * 2,
+        out_specs=(in_vmem, in_vmem),
+    )(applied, total)
+
+
 def fast_device(mesh_bands, orbitals, sphere_slot, stick_column, potential, subspace, previous):
     slots = sphere_slot.reshape(1, -1)
     columns = stick_column.reshape(1, -1)
-    return whole_work(mesh_bands, orbitals, slots, columns, potential, subspace, previous)
+    arrays = (orbitals, slots, columns, potential, subspace, previous)
+    applied, total = whole_work(mesh_bands, *arrays)
+    applied, turned = handed_out(mesh_bands, applied, total)
+    return applied, turned.transpose(0, 2, 1)
 
 
 def fits(mesh_bands, orbitals, slots, sticks, potential, subspace, previous):

time: 57.9 us -> 48.9 us (0.84)
  Pallas kernels: 54.1 us -> 48.1 us
  local copies, waits for them, and re-layouts: 2.88 us -> 0 us
    pallas_call x1, Pallas kernels: 54.1 us -> 46.6 us  [whole_work(): pl.pallas_call(functools.partial(whole_kernel, mesh_bands), out_shape=(ja...]
    unnamed x1 -> x0, local copies, waits for them, and re-layouts: 1.51 us -> none
    pallas_call x0 -> x1, Pallas kernels: none -> 1.51 us  [handed_out(): pl.pallas_call(functools.partial(hand_out, bands, mesh_bands * bands), ou...]
    pallas_call x1 -> x0, local copies, waits for them, and re-layouts: 1.37 us -> none  [whole_work(): pl.pallas_call(functools.partial(whole_kernel, mesh_bands), out_shape=(ja...]
where the time goes in v3:
time: 48.9 us; the launch traced here: 48.7 us
  Pallas kernels  48.1 us (98%)
  between operations  0.64 us (1%)
    pallas_call x1, Pallas kernels, whole_work(): pl.pallas_call(functools.partial(whole_kernel, mesh_bands), out_shape=(ja...  46.6 us
    pallas_call x1, Pallas kernels, handed_out(): pl.pallas_call(functools.partial(hand_out, bands, mesh_bands * bands), ou...  1.51 us

profile of v3, /device:TPU:0, one launch (start us, length us, event | category | flops | bytes accessed | tf_op | source)
XLA Modules:
  0.0 48.7 jit_solution(17168084671865353231)
XLA Ops:
  0.6 46.6 %shard_map.131 = (bf16[4,2,4096]{2,1,0:T(2,128)(2,1)}, f32[8,128]{1,0:T(8,128)}) custom-call(bf16[4,2,4096]{2,1,0:T(2,128)(2,1)} %orbital_ref.1, s32[1,4096]{1,0:T(1,128)} %bitcast.3, s32[1,128]{1,0:T(1,128)} %bitcast.5, bf16[4,2,4096]{2,1,0:T(2,128)(2,1)} %previous_ref.1, bf16[16,2,4096]{2,1,0:T(2,128)(2,1)} %subspace_hbm.1, f32[24,192,192]{2,1,0:T(8,128)} %pot_ref.1, ...), custom_call_target="tpu_custom_call" | custom-call | flops 40000000000 | bytes 8000000 | tf_op jit(solution)/shard_map/pallas_call | solution.py:780
  47.2 1.5 %shard_map.132 = (bf16[4,2,4096]{2,1,0:T(2,128)(2,1)}, f32[2,4,8]{2,1,0:T(4,128)}) custom-call(bf16[4,2,4096]{2,1,0:T(2,128)(2,1)} %get-tuple-element.6.applied_in, f32[8,128]{1,0:T(8,128)} %get-tuple-element.7.total_in), custom_call_target="tpu_custom_call" | custom-call | tf_op jit(solution)/shard_map/pallas_call | solution.py:857

commit v4 on v3

--- a/solution.py
+++ b/solution.py
@@ -196,10 +196,10 @@
 
 def whole_kernel(
     mesh_bands,
-    orbital_ref,
-    slot_ref,
-    column_ref,
-    previous_ref,
+    orbital_hbm,
+    slot_hbm,
+    column_hbm,
+    previous_hbm,
     subspace_hbm,
     pot_ref,
     deep_hbm,
@@ -207,9 +207,14 @@
     line_hbm,
     turn_hbm,
     half_hbm,
-    pick_ref,
+    pick_hbm,
     applied_ref,
     inter_ref,
+    orbital_ref,
+    slot_ref,
+    column_ref,
+    previous_ref,
+    pick_ref,
     subspace_ref,
     deep_ref,
     rise_ref,
@@ -239,6 +244,7 @@
     back_ref,
     every_ref,
     right_side_ref,
+    blend_ref,
     share_ref,
     shares_ref,
     load_sem,
@@ -316,12 +322,15 @@
     def await_bytes(region, sem):
         pltpu.make_async_copy(region, region, sem).wait()
 
-    def there_copy(group, place):
+    bounds = (0, 2, groups_pair, groups)
+
+    def there_copy(batch, place):
+        some = slice(bounds[batch], bounds[batch + 1])
         return remote(
-            sent_ref.at[group, others[place]],
-            stick_ref.at[group, me],
+            sent_ref.at[some, others[place]],
+            stick_ref.at[some, me],
             once_sem.at[6],
-            recv_sem.at[group],
+            recv_sem.at[batch],
             {"fft": others[place]},
         )
 
@@ -333,22 +342,6 @@
             home_recv.at[group],
             {"fft": others[place]},
         )
-
-    loads = []
-    for place, (src, dst) in enumerate(
-        (
-            (deep_hbm, deep_ref),
-            (line_hbm, line_ref),
-            (turn_hbm, turn_ref),
-            (subspace_hbm, subspace_ref),
-            (pot_ref, full_ref),
-            (pot_ref.at[:, :, :LANES], left_ref),
-            (half_hbm, half_ref),
-            (rise_hbm, rise_ref),
-        )
-    ):
-        loads.append(pltpu.make_async_copy(src, dst, load_sem.at[place]))
-        loads[-1].start()
 
     barrier = pltpu.get_barrier_semaphore()
     for place in range(mesh_bands):
@@ -361,6 +354,29 @@
                     device_id_type=pl.DeviceIdType.MESH,
                 )
 
+    loads = []
+    for place, (src, dst) in enumerate(
+        (
+            (slot_hbm, slot_ref),
+            (orbital_hbm, orbital_ref),
+            (column_hbm, column_ref),
+            (previous_hbm, previous_ref),
+            (deep_hbm, deep_ref),
+            (line_hbm, line_ref),
+            (turn_hbm, turn_ref),
+            (subspace_hbm, subspace_ref),
+            (pot_ref, full_ref),
+            (pot_ref.at[:, :, :LANES], left_ref),
+            (half_hbm, half_ref),
+            (pick_hbm, pick_ref),
+            (rise_hbm, rise_ref),
+        )
+    ):
+        loads.append(pltpu.make_async_copy(src, dst, load_sem.at[place]))
+        loads[-1].start()
+    for place in range(4):
+        loads[place].wait()
+
     low_lane = lax.broadcasted_iota(jnp.int32, (1, LANES), 1) < rest
     level = lax.broadcasted_iota(jnp.int32, (fold, LANES), 0)
     wave_ref[...] = orbital_ref[...].reshape(2 * bands, waves).astype(f32)
@@ -378,15 +394,17 @@
     def plane_of(block):
         return lax.shift_right_logical(slot_ref[:, lanes_of(block)], 7)
 
-    @pl.loop(0, blocks, unroll=4)
-    def _(block):
-        slot = slot_ref[:, lanes_of(block)]
+    def hot_of(block):
+        stick = jnp.bitwise_and(slot_ref[:, lanes_of(block)], sticks - 1)
         plane = plane_of(block)
-        cell = jnp.bitwise_and(slot, sticks - 1)
-        for side in range(1, FOLD):
-            cell = cell + jnp.where(plane >= side * fold, sticks, 0)
-        rows = lax.broadcasted_iota(jnp.int32, (FOLD * sticks, LANES), 0)
-        hot_ref[:, lanes_of(block)] = jnp.where(cell == rows, 1.0, 0.0).astype(bf16)
+        rows = lax.broadcasted_iota(jnp.int32, (sticks, LANES), 0)
+        chosen = jnp.where(stick == rows, 1.0, 0.0).astype(bf16).reshape(-1, 16, LANES)
+        sides = []
+        for side in range(FOLD):
+            inside = jnp.logical_and(plane >= side * fold, plane < (side + 1) * fold)
+            inside = jnp.broadcast_to(jnp.where(inside, 1.0, 0.0), (16, LANES)).astype(bf16)
+            sides.append((chosen * inside[None]).reshape(sticks, LANES))
+        return jnp.concatenate(sides, axis=0)
 
     pl.semaphore_wait(barrier, mesh_bands * owners - 1)
     for place in range(owners - 1):
@@ -405,6 +423,8 @@
     cells = None
     for block in range(0, blocks, 2):
         pieces = []
+        hot = jnp.concatenate([hot_of(block), hot_of(block + 1)], axis=1)
+        hot_ref[:, lanes_of(block, 2)] = hot
         for step in range(2):
             chosen = level_mask(block + step)
             values = wave_ref[:, lanes_of(block + step)]
@@ -413,7 +433,7 @@
         left = jnp.concatenate(pieces, axis=1).astype(bf16)
         term = lax.dot_general(
             left,
-            hot_ref[:, lanes_of(block, 2)],
+            hot,
             (((1,), (1,)), ((), ())),
             preferred_element_type=f32,
         )
@@ -427,7 +447,7 @@
                 pieces.append(cells[start : start + fold, side * LANES : (side + 1) * LANES])
         columns.append(jnp.concatenate(pieces, axis=0))
     columns = jnp.concatenate(columns, axis=1).astype(bf16)
-    loads[0].wait()
+    loads[4].wait()
     along = dot(deep_ref[...], columns).reshape(groups_pair * owners, 2 * PLANES, bands * LANES)
     for pair in range(pairs):
         chunks = []
@@ -439,27 +459,12 @@
             .reshape(groups_pair, owners, CHUNK, LANES)
         )
 
-    @pl.loop(0, groups)
-    def _(group):
+    for batch in range(2):
         for place in range(owners - 1):
-            there_copy(group, place).start()
-        stick_ref[group, me] = sent_ref[group, me]
-
-    freq_x = jnp.where(grid_x >= half, grid_x - size, grid_x)
-    freq_y = jnp.where(grid_y >= half, grid_y - size, grid_y)
-    freq_row = lax.broadcasted_iota(jnp.int32, (16, LANES), 0)
-    freqs = jnp.where(freq_row == 0, freq_x, jnp.where(freq_row == 1, freq_y, 0.0))
-    freqs = jnp.concatenate([freqs] * FOLD, axis=1).astype(bf16)
-
-    @pl.loop(0, blocks // 8)
-    def _(step):
-        found = dot(freqs, hot_ref[:, lanes_of(8 * step, 8)])
-        plane = lax.shift_right_logical(slot_ref[:, lanes_of(8 * step, 8)], 7)
-        freq_z = jnp.where(plane >= half, plane - size, plane).astype(f32)
-        total = freq_z * freq_z + found[0:1] * found[0:1] + found[1:2] * found[1:2]
-        kinetic_ref[:, lanes_of(8 * step, 8)] = total * (2.0 / (size * size))
-
-    for place in range(1, len(loads)):
+            there_copy(batch, place).start()
+    stick_ref[:, me] = sent_ref[:, me]
+
+    for place in range(5, len(loads)):
         loads[place].wait()
 
     @pl.loop(0, slab, unroll=4)
@@ -493,23 +498,22 @@
     await_bytes(every_ref.at[: mesh_bands - 1], once_sem.at[3])
 
     count = mesh_bands * bands
-    others_side = every_ref[...].reshape(count, 2, waves).astype(f32)
-    right_side_ref[:count] = others_side[:, 0].astype(bf16)
-    right_side_ref[count : 2 * count] = others_side[:, 1].astype(bf16)
-    own_side = subspace_ref[...].astype(f32)
-    own_side = jnp.concatenate([own_side[:, 0], own_side[:, 1]], axis=0).astype(bf16)
+    right_side_ref[: 2 * count] = every_ref[...].reshape(2 * count, waves)
     products = lax.dot_general(
-        own_side, right_side_ref[...], (((1,), (1,)), ((), ())), preferred_element_type=f32
+        subspace_ref[...].reshape(2 * mine, waves),
+        right_side_ref[...],
+        (((1,), (1,)), ((), ())),
+        preferred_element_type=f32,
     )
-    lane = lax.broadcasted_iota(jnp.int32, (1, LANES), 1)
-    upper, lower = products[:mine], products[mine:]
-    blend = jnp.where(
-        lane < count,
-        upper + pltpu.roll(lower, LANES - count, 1),
-        upper - pltpu.roll(lower, count, 1),
+    below = pltpu.roll(products, 2 * mine - 1, 0)
+    even_lane = jnp.bitwise_and(lax.broadcasted_iota(jnp.int32, (1, LANES), 1), 1) == 0
+    blend_ref[...] = jnp.where(
+        even_lane,
+        products + pltpu.roll(below, LANES - 1, 1),
+        products - pltpu.roll(below, 1, 1),
     )
     for block in range(shares):
-        share_ref[block] = blend[block * share : (block + 1) * share]
+        share_ref[block] = blend_ref[pl.ds(2 * share * block, share, 2), :]
 
     source_band = lax.div(me, shares)
     for block in range(shares):
@@ -657,40 +661,56 @@
                 part_row, found[:, :LANES], found[:, LANES:]
             ).astype(bf16)
 
-    def wait_group(group):
-        await_bytes(stick_ref.at[group, : owners - 1], recv_sem.at[group])
+    def wait_batch(batch):
+        some = slice(bounds[batch], bounds[batch + 1])
+        await_bytes(stick_ref.at[some, : owners - 1], recv_sem.at[batch])
 
     def send_home(group):
         for place in range(owners - 1):
             home_copy(group, place).start()
         back_ref[group, me] = stage_ref[group + 2, me]
 
-    wait_group(0)
+    for place in range(owners - 1):
+        there_copy(2, place).start()
+    wait_batch(0)
     spread_lines(0)
-
-    @pl.loop(0, groups)
+    for unit in range(PLANES // 2):
+        forward_lines(0, unit)
+    for unit in range(PLANES // 2):
+        backward_lines(unit)
+    spread_lines(1)
+
+    @pl.loop(1, groups - 1)
     def _(group):
-        @pl.when(group < groups - 1)
-        def _():
-            wait_group(group + 1)
-
-        forward_lines(group, 0)
-        forward_lines(group, 1)
+        for batch in (1, 2):
+
+            @pl.when(group + 1 == bounds[batch])
+            def _():
+                wait_batch(batch)
+
+        for unit in range(PLANES // 2):
+            forward_lines(group, unit)
         picked_lines(group)
         weighed_lines()
-        backward_lines(0)
-        backward_lines(1)
-        spread_lines(lax.rem(group + 1, groups))
+        for unit in range(PLANES // 2):
+            backward_lines(unit)
+        spread_lines(group + 1)
 
         @pl.when(group > 1)
         def _():
             send_home(group - 2)
 
+    for unit in range(PLANES // 2):
+        forward_lines(groups - 1, unit)
+    picked_lines(groups - 1)
+    weighed_lines()
+    for unit in range(PLANES // 2):
+        backward_lines(unit)
     picked_lines(groups)
     weighed_lines()
-    send_home(groups - 2)
     picked_lines(groups + 1)
-    send_home(groups - 1)
+    for group in range(groups - 3, groups):
+        send_home(group)
 
     def gather_waves(pair):
         first = pair * groups_pair
@@ -717,7 +737,7 @@
                 pieces.append(jnp.concatenate(sides, axis=1))
         gather_ref[...] = jnp.concatenate(pieces, axis=0)
 
-        @pl.loop(0, blocks // 2, unroll=4)
+        @pl.loop(0, blocks // 2, unroll=8)
         def _(step):
             values = dot(gather_ref[...], hot_ref[:, lanes_of(2 * step, 2)])
             for side in range(2):
@@ -729,7 +749,24 @@
                         jnp.where(chosen, ours, 0.0), axis=0, keepdims=True
                     )
 
+    def find_kinetic():
+        freq_x = jnp.where(grid_x >= half, grid_x - size, grid_x)
+        freq_y = jnp.where(grid_y >= half, grid_y - size, grid_y)
+        freq_row = lax.broadcasted_iota(jnp.int32, (16, LANES), 0)
+        freqs = jnp.where(freq_row == 0, freq_x, jnp.where(freq_row == 1, freq_y, 0.0))
+        freqs = jnp.concatenate([freqs] * FOLD, axis=1).astype(bf16)
+
+        @pl.loop(0, blocks // 8)
+        def _(step):
+            found = dot(freqs, hot_ref[:, lanes_of(8 * step, 8)])
+            plane = lax.shift_right_logical(slot_ref[:, lanes_of(8 * step, 8)], 7)
+            freq_z = jnp.where(plane >= half, plane - size, plane).astype(f32)
+            total = freq_z * freq_z + found[0:1] * found[0:1] + found[1:2] * found[1:2]
+            kinetic_ref[:, lanes_of(8 * step, 8)] = total * (2.0 / (size * size))
+
     for pair in range(pairs):
+        if pair == pairs - 1:
+            find_kinetic()
         gather_waves(pair)
 
     result = found_ref[...] + kinetic_ref[...] * wave_ref[...]
@@ -755,8 +792,11 @@
     total = shares_ref[0]
     for source in range(1, owners):
         total = total + shares_ref[source]
-    total = pltpu.roll(total, lax.rem(LANES - bands * band_me, LANES), 1)
-    inter_ref[...] = total
+    total = pltpu.roll(total, lax.rem(LANES - 2 * bands * band_me, LANES), 1).T
+    for part in range(2):
+        for band in range(bands):
+            row = 2 * band + part
+            inter_ref[part, band : band + 1, :] = total[row : row + 1]
 
 
 def whole_work(mesh_bands, orbitals, slots, columns, potential, subspace, previous):
@@ -780,12 +820,17 @@
     return pl.pallas_call(
         functools.partial(whole_kernel, mesh_bands),
         out_shape=(
-            jax.ShapeDtypeStruct(orbitals.shape, bf16),
-            jax.ShapeDtypeStruct((share, LANES), f32),
+            pltpu.VMEM(orbitals.shape, bf16),
+            pltpu.VMEM((2, bands, share), f32),
         ),
-        in_specs=[in_vmem] * 4 + [anywhere] * 7 + [in_vmem],
+        in_specs=[anywhere] * 12,
         out_specs=(in_vmem, in_vmem),
         scratch_shapes=[
+            pltpu.VMEM(orbitals.shape, bf16),
+            pltpu.VMEM(slots.shape, jnp.int32),
+            pltpu.VMEM(columns.shape, jnp.int32),
+            pltpu.VMEM(previous.shape, bf16),
+            pltpu.VMEM(pick.shape, bf16),
             pltpu.VMEM(subspace.shape, bf16),
             pltpu.VMEM(deep.shape, bf16),
             pltpu.VMEM(rise.shape, bf16),
@@ -815,10 +860,11 @@
             pltpu.VMEM((groups, owners, CHUNK, LANES), bf16),
             pltpu.VMEM((mesh_bands, bands, 2, waves), bf16),
             pltpu.VMEM((LANES, waves), bf16),
+            pltpu.VMEM((2 * mine, LANES), f32),
             pltpu.VMEM((mine // share, share, LANES), f32),
             pltpu.VMEM((owners, share, LANES), f32),
-            dma((8,)),
-            dma((groups,)),
+            dma((13,)),
+            dma((3,)),
             dma((groups,)),
             dma((8,)),
         ],
@@ -844,33 +890,11 @@
     )
 
 
-def hand_out(bands, count, applied_in, total_in, applied_ref, inter_ref):
-    applied_ref[...] = applied_in[...]
-    total = total_in[...].T
-    inter_ref[0] = total[:bands]
-    inter_ref[1] = total[count : count + bands]
-
-
-def handed_out(mesh_bands, applied, total):
-    bands, share = applied.shape[0], total.shape[0]
-    in_vmem = pl.BlockSpec(memory_space=pltpu.VMEM)
-    return pl.pallas_call(
-        functools.partial(hand_out, bands, mesh_bands * bands),
-        out_shape=(
-            jax.ShapeDtypeStruct(applied.shape, jnp.bfloat16),
-            jax.ShapeDtypeStruct((2, bands, share), jnp.float32),
-        ),
-        in_specs=[in_vmem] * 2,
-        out_specs=(in_vmem, in_vmem),
-    )(applied, total)
-
-
 def fast_device(mesh_bands, orbitals, sphere_slot, stick_column, potential, subspace, previous):
     slots = sphere_slot.reshape(1, -1)
     columns = stick_column.reshape(1, -1)
     arrays = (orbitals, slots, columns, potential, subspace, previous)
-    applied, total = whole_work(mesh_bands, *arrays)
-    applied, turned = handed_out(mesh_bands, applied, total)
+    applied, turned = whole_work(mesh_bands, *arrays)
     return applied, turned.transpose(0, 2, 1)
 
 

time: 48.9 us -> 46.3 us (0.947)
  Pallas kernels: 48.1 us -> 44.2 us
  local copies, waits for them, and re-layouts: 0 us -> 1.22 us
    pallas_call x2 -> x1, Pallas kernels: 48.1 us -> 44.2 us  [whole_work(): pl.pallas_call(functools.partial(whole_kernel, mesh_bands), out_shape=(pl...]
    unnamed x0 -> x2, local copies, waits for them, and re-layouts: none -> 1.22 us
where the time goes in v4:
time: 46.3 us; the launch traced here: 46 us
  Pallas kernels  44.2 us (95%)
  local copies, waits for them, and re-layouts  1.22 us (3%)
  between operations  0.64 us (1%)
    pallas_call x1, Pallas kernels, whole_work(): pl.pallas_call(functools.partial(whole_kernel, mesh_bands), out_shape=(pl...  44.2 us
    unnamed x2, local copies, waits for them, and re-layouts  1.22 us

profile of v4, /device:TPU:0, one launch (start us, length us, event | category | flops | bytes accessed | tf_op | source)
XLA Modules:
  0.0 46.0 jit_solution(14272700677758584689)
XLA Ops:
  0.6 44.2 %shard_map.131 = (bf16[4,2,4096]{2,1,0:T(2,128)(2,1)S(1)}, f32[2,4,8]{2,1,0:T(4,128)S(1)}) custom-call(bf16[4,2,4096]{2,1,0:T(2,128)(2,1)} %orbital_hbm.1, s32[1,4096]{1,0:T(1,128)} %bitcast.4, s32[1,128]{1,0:T(1,128)} %bitcast.5, bf16[4,2,4096]{2,1,0:T(2,128)(2,1)} %previous_hbm.1, bf16[16,2,4096]{2,1,0:T(2,128)(2,1)} %subspace_hbm.1, ...), custom_call_target="tpu_custom_call" | custom-call | flops 40000000000 | bytes 8000000 | tf_op jit(solution)/shard_map/pallas_call | solution.py:820
  44.8 0.6 %copy.16 = bf16[4,2,4096]{2,1,0:T(2,128)(2,1)} copy(bf16[4,2,4096]{2,1,0:T(2,128)(2,1)S(1)} %get-tuple-element.6) | data formatting | bytes 131072
  45.4 0.6 %copy.17 = f32[2,8,4]{1,2,0:T(4,128)} copy(f32[2,8,4]{1,2,0:T(4,128)S(1)} %bitcast.3) | data formatting | bytes 512

commit v5 on v4

--- a/solution.py
+++ b/solution.py
@@ -354,26 +354,25 @@
                     device_id_type=pl.DeviceIdType.MESH,
                 )
 
+    sides = (
+        (slot_hbm, slot_ref),
+        (orbital_hbm, orbital_ref),
+        (column_hbm, column_ref),
+        (previous_hbm, previous_ref),
+        (deep_hbm, deep_ref),
+        (line_hbm, line_ref),
+        (turn_hbm, turn_ref),
+        (subspace_hbm, subspace_ref),
+        (pot_ref, full_ref),
+        (half_hbm, half_ref),
+        (pick_hbm, pick_ref),
+        (rise_hbm, rise_ref),
+    )
     loads = []
-    for place, (src, dst) in enumerate(
-        (
-            (slot_hbm, slot_ref),
-            (orbital_hbm, orbital_ref),
-            (column_hbm, column_ref),
-            (previous_hbm, previous_ref),
-            (deep_hbm, deep_ref),
-            (line_hbm, line_ref),
-            (turn_hbm, turn_ref),
-            (subspace_hbm, subspace_ref),
-            (pot_ref, full_ref),
-            (pot_ref.at[:, :, :LANES], left_ref),
-            (half_hbm, half_ref),
-            (pick_hbm, pick_ref),
-            (rise_hbm, rise_ref),
-        )
-    ):
+    for place, (src, dst) in enumerate(sides):
         loads.append(pltpu.make_async_copy(src, dst, load_sem.at[place]))
-        loads[-1].start()
+    for place in range(5):
+        loads[place].start()
     for place in range(4):
         loads[place].wait()
 
@@ -406,11 +405,8 @@
             sides.append((chosen * inside[None]).reshape(sticks, LANES))
         return jnp.concatenate(sides, axis=0)
 
-    pl.semaphore_wait(barrier, mesh_bands * owners - 1)
-    for place in range(owners - 1):
-        coord_copy(place).start()
-    for place in range(mesh_bands - 1):
-        band_copy(place).start()
+    for place in range(5, len(loads)):
+        loads[place].start()
     coords_ref[me] = coord_ref[...]
     every_ref[band_me] = previous_ref[...]
 
@@ -459,9 +455,14 @@
             .reshape(groups_pair, owners, CHUNK, LANES)
         )
 
+    pl.semaphore_wait(barrier, mesh_bands * owners - 1)
+    for place in range(owners - 1):
+        coord_copy(place).start()
     for batch in range(2):
         for place in range(owners - 1):
             there_copy(batch, place).start()
+    for place in range(mesh_bands - 1):
+        band_copy(place).start()
     stick_ref[:, me] = sent_ref[:, me]
 
     for place in range(5, len(loads)):
@@ -471,6 +472,7 @@
     def _(plane):
         local = full_ref[plane, :, LANES:]
         right_ref[plane] = jnp.concatenate([local, local], axis=1)
+        left_ref[plane] = full_ref[plane, :, :LANES]
 
     await_bytes(coords_ref.at[: owners - 1], once_sem.at[1])
 
@@ -532,131 +534,117 @@
                     shares_ref[me] = share_ref[block]
 
     def spread_lines(group):
-        for low in range(half_owners):
-            results = []
-            for owner in (low, low + half_owners):
-                values = stick_ref[group, owner].astype(f32)
-                mask = mask_ref[owner]
-                parts = []
-                for part in range(2):
-                    pieces = []
-                    for plane in range(PLANES):
-                        for band in range(PAIR):
-                            row = band * 2 * PLANES + part * PLANES + plane
-                            pieces.append(values[row : row + 1, :] * mask)
-                    parts.append(jnp.concatenate(pieces, axis=0))
-                left = jnp.concatenate(parts, axis=1).astype(bf16)
-                results.append(dot(left, there_ref[owner]))
-            for plane in range(PLANES):
-                unit, side = plane // 2, plane % 2
-                start = plane * PAIR * slab
-
-                def pieces_of(result):
-                    one = result[start : start + slab]
-                    two = result[start + slab : start + 2 * slab]
-                    found = []
-                    for half_lines in (one, two):
-                        found.append((half_lines[:, :LANES], half_lines[:, LANES : 2 * LANES]))
-                    both = []
-                    for offset in (2 * LANES, 3 * LANES):
-                        both.append(
-                            jnp.where(
-                                low_lane,
-                                one[:, offset : offset + LANES],
-                                two[:, offset : offset + LANES],
-                            )
-                        )
-                    found.append(tuple(both))
-                    return found
-
-                near, far = pieces_of(results[0]), pieces_of(results[1])
-                offsets = (2 * side * LANES, (2 * side + 1) * LANES, (4 + side) * LANES)
-                for (near_re, near_im), (far_re, far_im), offset in zip(near, far, offsets):
-                    for parity in range(2):
-                        if parity == 0:
-                            real, imag = near_re + far_re, near_im + far_im
-                        else:
-                            real, imag = near_re - far_re, near_im - far_im
-                        tile = jnp.concatenate(
-                            [real.reshape(-1, 8, LANES), imag.reshape(-1, 8, LANES)], axis=1
-                        )
+        for owner in range(owners):
+            low, far = owner % half_owners, owner // half_owners
+            values = stick_ref[group, owner].astype(f32)
+            mask = mask_ref[owner]
+            parts = []
+            for part in range(2):
+                pieces = []
+                for plane in range(PLANES):
+                    for band in range(PAIR):
+                        row = band * 2 * PLANES + part * PLANES + plane
+                        pieces.append(values[row : row + 1, :] * mask)
+                parts.append(jnp.concatenate(pieces, axis=0))
+            left = jnp.concatenate(parts, axis=1).astype(bf16)
+            for tile in range(2):
+                place = slice(2 * LANES * tile, 2 * LANES * (tile + 1))
+                result = dot(left, there_ref[owner, :, place])
+                for plane in range(PLANES):
+                    unit, side = plane // 2, plane % 2
+                    start = plane * PAIR * slab
+                    for band in range(1 if tile else PAIR):
+                        found = []
+                        for part in range(2):
+                            here = slice(part * LANES, (part + 1) * LANES)
+                            one = result[start : start + slab, here]
+                            two = result[start + slab : start + 2 * slab, here]
+                            if tile:
+                                mine_here = jnp.where(low_lane, one, two)
+                            else:
+                                mine_here = two if band else one
+                            found.append(mine_here.reshape(-1, 8, LANES))
+                        offset = 4 + side if tile else 2 * side + band
                         mixed_ref[
-                            unit,
-                            parity,
-                            slice(2 * slab * low, 2 * slab * (low + 1)),
-                            offset : offset + LANES,
-                        ] = tile.reshape(2 * slab, LANES).astype(bf16)
+                            unit, far, offset, 2 * slab * low : 2 * slab * (low + 1)
+                        ] = jnp.concatenate(found, axis=1).reshape(2 * slab, LANES).astype(bf16)
 
     def forward_lines(group, unit):
         first = lax.rem(group, groups_pair) * PLANES
-        if True:
+        for tile in range(3):
+            near, far = [
+                jnp.concatenate(
+                    [mixed_ref[unit, side, 2 * tile], mixed_ref[unit, side, 2 * tile + 1]], axis=1
+                )
+                for side in range(2)
+            ]
             for parity in range(2):
                 picks = pl.ds(parity, half, 2)
-
-                for tile in range(3):
-                    result = dot(
-                        half_ref[parity],
-                        mixed_ref[unit, parity, :, 2 * LANES * tile : 2 * LANES * (tile + 1)],
-                    )
-                    if tile < 2:
-                        local = left_ref[first + 2 * unit + tile, picks, :]
-                        local = jnp.concatenate([local, local], axis=1)
-                    else:
-                        one = right_ref[first + 2 * unit, picks, :]
-                        two = right_ref[first + 2 * unit + 1, picks, :]
-                        local = jnp.concatenate([one, two], axis=1)
-                    heavy_ref[unit, parity, tile, :half] = (result[:half] * local).astype(bf16)
-                    heavy_ref[unit, parity, tile, half:] = (result[half:] * local).astype(bf16)
+                result = dot(half_ref[parity], near - far if parity else near + far)
+                if tile < 2:
+                    one = left_ref[first + 2 * unit + tile, picks, :]
+                    two = one
+                else:
+                    one = right_ref[first + 2 * unit, picks, :]
+                    two = right_ref[first + 2 * unit + 1, picks, :]
+                for side, local in enumerate((one, two)):
+                    here = slice(side * LANES, (side + 1) * LANES)
+                    for part in range(2):
+                        rows = slice(part * half, (part + 1) * half)
+                        heavy_ref[unit, parity, tile, side, rows] = (
+                            result[rows, here] * local
+                        ).astype(bf16)
 
     def backward_lines(unit):
-        if True:
-            for tile in range(3):
-                even = dot(half_ref[2], heavy_ref[unit, 0, tile])
-                odd = dot(half_ref[3], heavy_ref[unit, 1, tile])
-                for side, values in enumerate((even + odd, even - odd)):
+        for tile in range(3):
+            for parity in range(2):
+                heavy = jnp.concatenate(
+                    [heavy_ref[unit, parity, tile, 0], heavy_ref[unit, parity, tile, 1]], axis=1
+                )
+                values = dot(half_ref[2 + parity], heavy)
+                for part in range(2):
                     for low in range(half_owners):
-                        owner = low + side * half_owners
-                        for part in range(2):
-                            start = part * half + low * slab
-                            found = values[start : start + slab]
-                            one, two = found[:, :LANES], found[:, LANES:]
-                            if tile < 2:
-                                rows = pl.ds(
-                                    pl.multiple_of((2 * unit + tile) * 2 * slab, 2 * slab), 2 * slab
-                                )
-                                after_ref[owner, rows, part * LANES : (part + 1) * LANES] = (
-                                    jnp.concatenate([one, two], axis=0).astype(bf16)
-                                )
-                            else:
-                                for place, both in enumerate((one, two)):
-                                    plane = 2 * unit + place
-                                    rows = pl.ds(
-                                        pl.multiple_of(plane * 2 * slab, 2 * slab), 2 * slab
-                                    )
-                                    after_ref[
-                                        owner, rows, (2 + part) * LANES : (3 + part) * LANES
-                                    ] = jnp.concatenate(
-                                        [
-                                            jnp.where(low_lane, both, 0.0),
-                                            jnp.where(low_lane, 0.0, both),
-                                        ],
-                                        axis=0,
-                                    ).astype(bf16)
+                        start = part * half + low * slab
+                        found = values[start : start + slab]
+                        one, two = found[:, :LANES], found[:, LANES:]
+                        if tile < 2:
+                            plane = 2 * unit + tile
+                            after_ref[
+                                parity, low, part, plane * 2 * slab : (plane + 1) * 2 * slab
+                            ] = jnp.concatenate([one, two], axis=0).astype(bf16)
+                            continue
+                        for place, both in enumerate((one, two)):
+                            plane = 2 * unit + place
+                            after_ref[
+                                parity, low, 2 + part, plane * 2 * slab : (plane + 1) * 2 * slab
+                            ] = jnp.concatenate(
+                                [jnp.where(low_lane, both, 0.0), jnp.where(low_lane, 0.0, both)],
+                                axis=0,
+                            ).astype(bf16)
 
     part_row = lax.broadcasted_iota(jnp.int32, (CHUNK, LANES), 0)
     part_row = jnp.bitwise_and(part_row, PLANES) == 0
 
     def weighed_lines():
-        for owner in range(owners):
-            result = dot(after_ref[owner], again_ref[owner])
-            mask = mask_ref[owner] * scale
-            mask = jnp.concatenate([mask, mask], axis=1)[None]
-            kept = (result.reshape(lines, slab, 2 * LANES) * mask).reshape(lines * slab, 2 * LANES)
-            kept_ref[owner] = kept.astype(bf16)
+        for low in range(half_owners):
+            even, odd = [
+                jnp.concatenate([after_ref[parity, low, lane] for lane in range(4)], axis=1)
+                for parity in range(2)
+            ]
+            for side in range(2):
+                owner = low + side * half_owners
+                result = dot(even - odd if side else even + odd, again_ref[owner])
+                mask = mask_ref[owner] * scale
+                for part in range(2):
+                    kept = result[:, part * LANES : (part + 1) * LANES].reshape(lines, slab, LANES)
+                    kept_ref[owner, part] = (
+                        (kept * mask[None]).reshape(lines * slab, LANES).astype(bf16)
+                    )
 
     def picked_lines(place):
         for owner in range(owners):
-            found = dot(pick_ref[...], kept_ref[owner])
+            kept = jnp.concatenate([kept_ref[owner, 0], kept_ref[owner, 1]], axis=1)
+            found = dot(pick_ref[...], kept)
             stage_ref[place, owner] = jnp.where(
                 part_row, found[:, :LANES], found[:, LANES:]
             ).astype(bf16)
@@ -852,10 +840,10 @@
             pltpu.VMEM((owners, slab, LANES), f32),
             pltpu.VMEM((owners, 2 * LANES, 4 * LANES), bf16),
             pltpu.VMEM((owners, 4 * LANES, 2 * LANES), bf16),
-            pltpu.VMEM((PLANES // 2, 2, size, 6 * LANES), bf16),
-            pltpu.VMEM((PLANES // 2, 2, 3, size, 2 * LANES), bf16),
-            pltpu.VMEM((owners, lines * slab, 4 * LANES), bf16),
-            pltpu.VMEM((owners, lines * slab, 2 * LANES), bf16),
+            pltpu.VMEM((PLANES // 2, 2, 6, size, LANES), bf16),
+            pltpu.VMEM((PLANES // 2, 2, 3, 2, size, LANES), bf16),
+            pltpu.VMEM((2, owners // 2, 4, lines * slab, LANES), bf16),
+            pltpu.VMEM((owners, 2, lines * slab, LANES), bf16),
             pltpu.VMEM((groups + 2, owners, CHUNK, LANES), bf16),
             pltpu.VMEM((groups, owners, CHUNK, LANES), bf16),
             pltpu.VMEM((mesh_bands, bands, 2, waves), bf16),
@@ -863,7 +851,7 @@
             pltpu.VMEM((2 * mine, LANES), f32),
             pltpu.VMEM((mine // share, share, LANES), f32),
             pltpu.VMEM((owners, share, LANES), f32),
-            dma((13,)),
+            dma((12,)),
             dma((3,)),
             dma((groups,)),
             dma((8,)),

time: 46.3 us -> 45.8 us (0.989)
  Pallas kernels: 44.2 us -> 43.7 us
    pallas_call x1, Pallas kernels: 44.2 us -> 43.7 us  [whole_work(): pl.pallas_call(functools.partial(whole_kernel, mesh_bands), out_shape=(pl...]
where the time goes in v5:
time: 45.8 us; the launch traced here: 45.5 us
  Pallas kernels  43.7 us (95%)
  local copies, waits for them, and re-layouts  1.22 us (3%)
  between operations  0.64 us (1%)
    pallas_call x1, Pallas kernels, whole_work(): pl.pallas_call(functools.partial(whole_kernel, mesh_bands), out_shape=(pl...  43.7 us
    unnamed x2, local copies, waits for them, and re-layouts  1.22 us

profile of v5, /device:TPU:0, one launch (start us, length us, event | category | flops | bytes accessed | tf_op | source)
XLA Modules:
  0.0 45.5 jit_solution(3751261053810215988)
XLA Ops:
  0.6 43.7 %shard_map.131 = (bf16[4,2,4096]{2,1,0:T(2,128)(2,1)S(1)}, f32[2,4,8]{2,1,0:T(4,128)S(1)}) custom-call(bf16[4,2,4096]{2,1,0:T(2,128)(2,1)} %orbital_hbm.1, s32[1,4096]{1,0:T(1,128)} %bitcast.4, s32[1,128]{1,0:T(1,128)} %bitcast.5, bf16[4,2,4096]{2,1,0:T(2,128)(2,1)} %previous_hbm.1, bf16[16,2,4096]{2,1,0:T(2,128)(2,1)} %subspace_hbm.1, ...), custom_call_target="tpu_custom_call" | custom-call | flops 40000000000 | bytes 8000000 | tf_op jit(solution)/shard_map/pallas_call | solution.py:808
  44.3 0.6 %copy.16 = bf16[4,2,4096]{2,1,0:T(2,128)(2,1)} copy(bf16[4,2,4096]{2,1,0:T(2,128)(2,1)S(1)} %get-tuple-element.6) | data formatting | bytes 131072
  44.9 0.6 %copy.17 = f32[2,8,4]{1,2,0:T(4,128)} copy(f32[2,8,4]{1,2,0:T(4,128)S(1)} %bitcast.3) | data formatting | bytes 512
